TPU v7x, 128 devices: a whole 4x4x4 slice. The times are simulated.
128 devices in a mesh: aa: 16 (over z_hi, x, core), ba: 8 (over z_lo, y).
Axes of the slice: x: 4, y: 4, z: 4 (z_hi: 2, z_lo: 2; z = z_hi * 2 + z_lo), core: 2. Of those that a mesh axis runs over, the one named last changes fastest.
Arguments:
- images: float32 [128, 4, 128, 4096], P(('aa', 'ba')), may hold values from 0 to 0.06, as said below
- depth: int32 [128], replicated, may hold values from 0 to 127, as said below
- brick_map: int32 [128], replicated, may hold values from 0 to 127, as said below
Outputs:
- composite: float32 [4, 128, 4096], replicated
Inputs may be any that keep to these rules, and one draw needn't show every extreme that they name: depth: a permutation of 0 to 127; the devices that share one index of ba hold bricks of 16 consecutive depth ranks. brick_map: a permutation of 0 to 127. images: channel 3 (alpha) lies between 0.002 and 0.06; channels 0 to 2 lie between 0 and the pixel's alpha.
All inputs are finite; a program needn't handle non-finite values.
Results may differ from a plain program's by a relative error of at most 0.00002.
Values sent between devices are 32-bit elements; how exact they have to be, the bound alone decides.
A program may use at most 128 MiB of HBM per device.

v0:
```python
import jax
import jax.numpy as jnp
from jax import lax
from jax.sharding import Mesh
from jax.sharding import PartitionSpec as P

AA = ("aa_0", "aa_1", "aa_2")
BA = ("ba_0", "ba_1")
AA_BA = ("aa_0", "aa_1", "aa_2", "ba_0", "ba_1")


def cut_rows(length, count):
    unit = 8 if length >= 8 * count else 1
    return [length // unit * k // count * unit for k in range(1, count)]


def gather_in_order(array, axes, turns):
    pieces = array
    for k in turns:
        pieces = lax.all_gather(pieces, axes[k])
    done = turns[::-1]
    back = [done.index(k) for k in range(len(axes))]
    pieces = pieces.transpose(*back, *range(len(axes), pieces.ndim))
    return pieces.reshape(-1, *array.shape)


def laid_out(pieces, dim):
    pieces = jnp.moveaxis(pieces, 0, dim)
    lengths = pieces.shape
    return pieces.reshape(*lengths[:dim], lengths[dim] * lengths[dim + 1], *lengths[dim + 2 :])


def gather_all_axes(array, axes, dim):
    numbers = list(range(len(axes)))[::-1]
    cut = array.shape.index(max(array.shape[:-1] or array.shape))
    edges = [0, *cut_rows(array.shape[cut], len(axes)), array.shape[cut]]
    outs = []
    for k, (start, end) in enumerate(zip(edges, edges[1:])):
        if end > start:
            piece = lax.slice_in_dim(array, start, end, axis=cut)
            outs.append(gather_in_order(piece, axes, numbers[k:] + numbers[:k]))
    return laid_out(jnp.concatenate(outs, axis=cut + 1), dim)


def blend_ordered(stacked, ordering):
    channels = stacked.shape[0]
    count = stacked.shape[1]
    rows = stacked.shape[2]
    columns = stacked.shape[3]
    ordered = jnp.take(stacked, ordering, axis=1)
    layers = jnp.moveaxis(ordered.reshape(channels, count, rows * columns), 1, 0)
    while layers.shape[0] > 1:
        front = layers[0::2]
        behind = layers[1::2]
        layers = front + (1.0 - front[:, 3:4]) * behind
    return layers[0].reshape(channels, rows, columns)


def local(images, depth, brick_map):
    picture = images[0]
    count_a = lax.axis_size(AA)
    count_b = lax.axis_size(BA)
    devices = count_a * count_b
    rows = picture.shape[1]
    columns = picture.shape[2]
    bricks = jnp.arange(devices, dtype=jnp.int32)
    matches = brick_map[:, None] == bricks[None, :]
    device_rank = jnp.sum(jnp.where(matches, depth[None, :], 0), axis=1)
    rank_table = device_rank.reshape(count_a, count_b)
    index_b = lax.axis_index(BA)
    bands = picture.reshape(4, count_a, rows // count_a, columns)
    received = lax.all_to_all(bands, AA, split_axis=1, concat_axis=1, tiled=True)
    group_ranks = lax.dynamic_index_in_dim(rank_table, index_b, 1, keepdims=False)
    partial_value = blend_ordered(received, jnp.argsort(group_ranks))
    pieces = partial_value.reshape(4, count_b, rows // devices, columns)
    second = lax.all_to_all(pieces, BA, split_axis=1, concat_axis=1, tiled=True)
    group_front = jnp.min(rank_table, axis=0)
    strip = blend_ordered(second, jnp.argsort(group_front))
    return gather_all_axes(strip, AA_BA, 1)


def solution(mesh):
    torus = Mesh(mesh.devices.reshape(2, 4, 2, 2, 4), ("aa_0", "aa_1", "aa_2", "ba_0", "ba_1"))
    return jax.shard_map(
        local,
        mesh=torus,
        in_specs=(P(AA_BA, None, None, None), P(), P()),
        out_specs=P(),
        check_vma=False,
    )
```

profile of v0, /device:TPU:1, one launch (start us, length us, event | category | flops | bytes accessed | tf_op | source)
XLA Modules:
  0.0 426.3 jit_solution(920055903281346040)
XLA Ops:
  6.5 7.8 %copy.70 = f32[4,16,8,4096]{3,2,0,1:T(8,128)} copy(f32[4,16,8,4096]{3,2,1,0:T(8,128)} %bitcast.71) | data formatting | bytes 16777216 | tf_op jit(solution)/shard_map/reshape;squeeze | solution.py:71
  14.3 9.2 %all-to-all-start = ((f32[4,16,8,4096]{3,2,0,1:T(8,128)}), f32[4,16,8,4096]{3,2,0,1:T(8,128)}, u32[]{:S(2)}, u32[]{:S(2)}) async-start(f32[4,16,8,4096]{3,2,0,1:T(8,128)} %copy.70), calls=%async_computation | async-start | bytes 16777216 | tf_op jit(solution)/shard_map/all_to_all | solution.py:72
  26.2 109.8 %all-to-all-done = f32[4,16,8,4096]{3,2,0,1:T(8,128)} async-done(((f32[4,16,8,4096]{3,2,0,1:T(8,128)}), f32[4,16,8,4096]{3,2,0,1:T(8,128)}, u32[]{:S(2)}, u32[]{:S(2)}) %all-to-all-start) | async-done | bytes 8388640 | tf_op jit(solution)/shard_map/all_to_all | solution.py:72
  136.0 7.9 %gather_fusion = f32[16,4,8,4096]{3,2,1,0:T(8,128)} fusion(f32[4,16,8,4096]{3,2,0,1:T(8,128)} %all-to-all-done, s32[1024]{0:T(1024)S(1)} %pad_clamp_fusion.1), kind=kCustom, calls=%fused_computation | custom fusion | bytes 16777280 | tf_op jit(solution)/shard_map/jit(_take)/gather | solution.py:50
  143.9 10.8 %gather.13 = f32[4,16,32768]{2,0,1:T(4,128)} reshape(f32[4,16,8,4096]{3,2,0,1:T(8,128)} %bitcast.70) | data formatting | bytes 16777216 | tf_op jit(solution)/shard_map/jit(_take)/gather | solution.py:50
  154.7 9.7 %select_bitcast_fusion = f32[16,4,32768]{2,1,0:T(4,128)} fusion(f32[4,16,32768]{2,0,1:T(4,128)} %gather.13, pred[16]{0:T(512)(128)(4,1)S(1)} %compare_and_fusion), kind=kLoop, calls=%fused_computation.4 | loop fusion | flops 2097152 | bytes 16777232 | tf_op jit(solution)/shard_map/transpose | solution.py:51
  179.6 10.0 %all-to-all-done.1 = f32[4,8,1,4096]{3,0,2,1:T(4,128)S(1)} async-done(((f32[4,8,1,4096]{3,0,2,1:T(4,128)}), f32[4,8,1,4096]{3,0,2,1:T(4,128)S(1)}, u32[]{:S(2)}, u32[]{:S(2)}) %all-to-all-start.1) | async-done | bytes 524320 | tf_op jit(solution)/shard_map/all_to_all | solution.py:76
  191.2 9.1 %all-gather.10 = f32[4,1,4096]{2,1,0:T(1,128)S(1)} all-gather(f32[1,1,4096]{2,1,0:T(1,128)S(1)} %get-tuple-element.11), channel_id=12, replica_groups=mesh['aa_0'=2,'aa_1'=4,'aa_2'=2,'ba_0'=2,'ba_1'=4] {'aa_1'}, dimensions={0}, use_global_device_ids=true | all-gather | bytes 81920 | tf_op jit(solution)/shard_map/all_gather | solution.py:20
  200.4 5.3 %all-gather.11 = f32[8,1,4096]{2,1,0:T(1,128)S(1)} all-gather(f32[4,1,4096]{2,1,0:T(1,128)S(1)} %all-gather.10), channel_id=13, replica_groups=mesh['aa_0'=2,'aa_1'=4,'aa_2'=2,'ba_0'=2,'ba_1'=4] {'aa_0'}, dimensions={0}, use_global_device_ids=true | all-gather | bytes 196608 | tf_op jit(solution)/shard_map/all_gather | solution.py:20
  205.7 10.9 %all-gather.12 = f32[8,4,1,1,4096]{4,1,3,2,0:T(4,128)} all-gather(f32[2,4,1,1,4096]{4,1,3,2,0:T(4,128)S(1)} %copy.81), channel_id=14, replica_groups=mesh['aa_0'=2,'aa_1'=4,'aa_2'=2,'ba_0'=2,'ba_1'=4] {'ba_1'}, dimensions={0}, use_global_device_ids=true | all-gather | bytes 655360 | tf_op jit(solution)/shard_map/all_gather | solution.py:20
  216.7 9.0 %all-gather.5 = f32[2,1,4096]{2,1,0:T(1,128)S(1)} all-gather(f32[1,1,4096]{2,1,0:T(1,128)S(1)} %get-tuple-element.12), channel_id=7, replica_groups=mesh['aa_0'=2,'aa_1'=4,'aa_2'=2,'ba_0'=2,'ba_1'=4] {'aa_2'}, dimensions={0}, use_global_device_ids=true | all-gather | bytes 49152 | tf_op jit(solution)/shard_map/all_gather | solution.py:20
  225.7 9.1 %all-gather.6 = f32[8,1,4096]{2,1,0:T(1,128)S(1)} all-gather(f32[2,1,4096]{2,1,0:T(1,128)S(1)} %all-gather.5), channel_id=8, replica_groups=mesh['aa_0'=2,'aa_1'=4,'aa_2'=2,'ba_0'=2,'ba_1'=4] {'aa_1'}, dimensions={0}, use_global_device_ids=true | all-gather | bytes 163840 | tf_op jit(solution)/shard_map/all_gather | solution.py:20
  235.0 9.8 %all-gather.7 = f32[8,2,1,1,4096]{4,1,3,2,0:T(2,128)S(1)} all-gather(f32[4,2,1,1,4096]{4,1,3,2,0:T(2,128)S(1)} %copy.76), channel_id=9, replica_groups=mesh['aa_0'=2,'aa_1'=4,'aa_2'=2,'ba_0'=2,'ba_1'=4] {'aa_0'}, dimensions={0}, use_global_device_ids=true | all-gather | bytes 393216 | tf_op jit(solution)/shard_map/all_gather | solution.py:20
  250.7 9.1 %all-gather.16 = f32[8,1,4096]{2,1,0:T(1,128)S(1)} all-gather(f32[2,1,4096]{2,1,0:T(1,128)S(1)} %all-gather.15), channel_id=18, replica_groups=mesh['aa_0'=2,'aa_1'=4,'aa_2'=2,'ba_0'=2,'ba_1'=4] {'ba_1'}, dimensions={0}, use_global_device_ids=true | all-gather | bytes 163840 | tf_op jit(solution)/shard_map/all_gather | solution.py:20
  264.6 10.8 %all-gather.18 = f32[4,4,2,1,1,4096]{5,1,4,3,2,0:T(4,128)} all-gather(f32[2,4,2,1,1,4096]{5,1,4,3,2,0:T(4,128)S(1)} %copy.86), channel_id=20, replica_groups=mesh['aa_0'=2,'aa_1'=4,'aa_2'=2,'ba_0'=2,'ba_1'=4] {'aa_2'}, dimensions={0}, use_global_device_ids=true | all-gather | bytes 786432 | tf_op jit(solution)/shard_map/all_gather | solution.py:20
  282.3 9.9 %all-gather.2 = f32[8,2,1,1,4096]{4,1,3,2,0:T(2,128)S(1)} all-gather(f32[2,2,1,1,4096]{4,1,3,2,0:T(2,128)S(1)} %copy.71), channel_id=4, replica_groups=mesh['aa_0'=2,'aa_1'=4,'aa_2'=2,'ba_0'=2,'ba_1'=4] {'aa_1'}, dimensions={0}, use_global_device_ids=true | all-gather | bytes 327680 | tf_op jit(solution)/shard_map/all_gather | solution.py:20
  292.3 7.4 %all-gather.3 = f32[8,2,2,1,1,4096]{5,2,4,3,1,0:T(2,128)S(1)} all-gather(f32[4,2,2,1,1,4096]{5,2,4,3,1,0:T(2,128)S(1)} %bitcast.86), channel_id=5, replica_groups=mesh['aa_0'=2,'aa_1'=4,'aa_2'=2,'ba_0'=2,'ba_1'=4] {'aa_0'}, dimensions={0}, use_global_device_ids=true | all-gather | bytes 786432 | tf_op jit(solution)/shard_map/all_gather | solution.py:20
  301.5 8.3 %all-gather.37.cloned.1.call-done = f32[8,2,4,2,1,1,4096]{6,2,5,4,3,1,0:T(4,128)} async-done(((f32[2,2,4,2,1,1,4096]{6,2,5,4,3,1,0:T(4,128)}), f32[8,2,4,2,1,1,4096]{6,2,5,4,3,1,0:T(4,128)}) %all-gather.37.cloned.1.call-update) | async-done | bytes 2097168 | tf_op jit(solution)/shard_map/all_gather | solution.py:20
  313.5 11.0 %all-gather.35.cloned.1.call-done = f32[4,4,2,4,1,1,4096]{6,3,5,4,2,1,0:T(4,128)} async-done(((f32[2,4,2,4,1,1,4096]{6,3,5,4,2,1,0:T(4,128)}), f32[4,4,2,4,1,1,4096]{6,3,5,4,2,1,0:T(4,128)}) %all-gather.35.cloned.1.call-update) | async-done | bytes 2097168 | tf_op jit(solution)/shard_map/all_gather | solution.py:20
  324.5 5.1 %copy.84 = f32[2,2,4,2,4,1,1,4096]{7,6,5,2,1,0,4,3:T(1,128)} copy(f32[2,2,4,2,4,1,1,4096]{7,4,3,2,1,0,6,5:T(4,128)} %bitcast.80) | data formatting | bytes 4194304 | tf_op jit(solution)/shard_map/all_gather | solution.py:20
  329.6 28.0 %all-gather.27.cloned.1.call-done = f32[8,4,2,2,1,1,4096]{6,1,5,4,3,2,0:T(4,128)} async-done(((f32[2,4,2,2,1,1,4096]{6,1,5,4,3,2,0:T(4,128)}), f32[8,4,2,2,1,1,4096]{6,1,5,4,3,2,0:T(4,128)}) %all-gather.27.cloned.1.call-update) | async-done | bytes 2097168 | tf_op jit(solution)/shard_map/all_gather | solution.py:20
  364.4 30.4 %all-gather.31.cloned.1.call-done = f32[8,2,4,2,1,1,4096]{6,2,5,4,3,1,0:T(4,128)} async-done(((f32[4,2,4,2,1,1,4096]{6,2,5,4,3,1,0:T(4,128)}), f32[8,2,4,2,1,1,4096]{6,2,5,4,3,1,0:T(4,128)}) %all-gather.31.cloned.1.call-update) | async-done | bytes 2097168 | tf_op jit(solution)/shard_map/all_gather | solution.py:20
  398.8 9.1 %maximum_bitcast_fusion = f32[4,128,1,4096]{3,2,1,0:T(1,128)S(1)} fusion(f32[128,1,1,4096]{3,2,0,1:T(1,128)S(1)} %bitcast.73, f32[128,1,1,4096]{3,2,0,1:T(1,128)S(1)} %bitcast.74, f32[128,1,1,4096]{3,2,0,1:T(1,128)S(1)} %bitcast.76, f32[128,1,1,4096]{3,2,0,1:T(1,128)S(1)} %bitcast.75), kind=kLoop, calls=%fused_computation.2 | loop fusion | flops 6291456 | bytes 16777216 | tf_op jit(solution)/shard_map/transpose | solution.py:28
  407.9 11.5 %copy.103 = f32[4,128,1,4096]{3,1,2,0:T(8,128)} copy(f32[4,128,1,4096]{3,2,1,0:T(1,128)S(1)} %maximum_bitcast_fusion) | data formatting | bytes 16777216
  (81 shorter events, 53.4 us)
Async XLA Ops:
  14.3 9.3 %copy-start.3 = (s32[128]{0:T(128)S(1)}, s32[128]{0:T(128)}, u32[]{:S(2)}) copy-start(s32[128]{0:T(128)} %param.4) | copy-start | bytes 1540
  14.3 9.3 %copy-start.4 = (s32[128]{0:T(128)S(1)}, s32[128]{0:T(128)}, u32[]{:S(2)}) copy-start(s32[128]{0:T(128)} %param.5) | copy-start | bytes 1540
  14.3 121.7 %all-to-all-start = ((f32[4,16,8,4096]{3,2,0,1:T(8,128)}), f32[4,16,8,4096]{3,2,0,1:T(8,128)}, u32[]{:S(2)}, u32[]{:S(2)}) async-start(f32[4,16,8,4096]{3,2,0,1:T(8,128)} %copy.70), calls=%async_computation | async-start | bytes 16777216 | tf_op jit(solution)/shard_map/all_to_all | solution.py:72
  164.4 4.6 %copy-start = (f32[16,4,32768]{2,1,0:T(4,128)S(1)}, f32[16,4,32768]{2,1,0:T(4,128)}, u32[]{:S(2)}) copy-start(f32[16,4,32768]{2,1,0:T(4,128)} %select_bitcast_fusion) | copy-start | bytes 25165828
  174.7 14.9 %all-to-all-start.1 = ((f32[4,8,1,4096]{3,0,2,1:T(4,128)}), f32[4,8,1,4096]{3,0,2,1:T(4,128)S(1)}, u32[]{:S(2)}, u32[]{:S(2)}) async-start(f32[4,8,1,4096]{3,0,2,1:T(4,128)} %bitcast.4), calls=%async_computation.1 | async-start | bytes 1048576 | tf_op jit(solution)/shard_map/all_to_all | solution.py:76
  179.4 96.1 %all-gather.33.cloned.1.call-start = ((), (), s32[]{:S(2)}) async-start(), calls=%async_computation.5 | async-start | bytes 1572864 | tf_op jit(solution)/shard_map/all_gather | solution.py:20
  216.7 84.3 %all-gather.29.cloned.1.call-start = ((), (), s32[]{:S(2)}) async-start(), calls=%async_computation.3 | async-start | bytes 1310720 | tf_op jit(solution)/shard_map/all_gather | solution.py:20
  245.6 64.1 %all-gather.37.cloned.1.call-start = ((), (), s32[]{:S(2)}) async-start(), calls=%async_computation.7 | async-start | bytes 2621440 | tf_op jit(solution)/shard_map/all_gather | solution.py:20
  275.4 49.1 %all-gather.35.cloned.1.call-start = ((), (), s32[]{:S(2)}) async-start(), calls=%async_computation.6 | async-start | bytes 3145728 | tf_op jit(solution)/shard_map/all_gather | solution.py:20
  276.0 81.6 %all-gather.27.cloned.1.call-start = ((), (), s32[]{:S(2)}) async-start(), calls=%async_computation.2 | async-start | bytes 2621440 | tf_op jit(solution)/shard_map/all_gather | solution.py:20
  300.9 93.9 %all-gather.31.cloned.1.call-start = ((), (), s32[]{:S(2)}) async-start(), calls=%async_computation.4 | async-start | bytes 3145728 | tf_op jit(solution)/shard_map/all_gather | solution.py:20
  394.8 3.9 copy-start.1
  394.8 3.9 copy-start.2
Sparse Core Ops, SparseCore 0:
  216.8 32.3 all-gather.32
  250.8 23.0 all-gather.28
  275.6 34.1 all-gather.36
  311.3 13.2 all-gather.34
  326.0 31.5 all-gather.26
  359.1 35.6 all-gather.30
where the time goes:
time: 427 us; the launch traced here: 426 us
  waiting for transfers between devices  199 us (47%)
  blocking collectives  106 us (25%)
  local copies, waits for them, and re-layouts  65.4 us (15%)
  other arithmetic  27.9 us (7%)
  starting transfers between devices  14.3 us (3%)
  between operations  13.8 us (3%)
    all_to_all x1, waiting for transfers between devices, local(): lax.all_to_all(bands, AA, split_axis=1, concat_axis=1, tiled=True)  110 us
    all_gather x14, blocking collectives, gather_in_order(): pieces = lax.all_gather(pieces, axes[k])  106 us
    all_gather x6, waiting for transfers between devices, gather_in_order(): pieces = lax.all_gather(pieces, axes[k])  77.7 us
    gather x3, local copies, waits for them, and re-layouts, blend_ordered(): ordered = jnp.take(stacked, ordering, axis=1)  19.6 us
    all_gather x11, local copies, waits for them, and re-layouts, gather_in_order(): pieces = lax.all_gather(pieces, axes[k])  18.5 us
    unnamed x16, local copies, waits for them, and re-layouts  12.8 us
    all_to_all x1, waiting for transfers between devices, local(): second = lax.all_to_all(pieces, BA, split_axis=1, concat_axis=1, tiled=True)  9.98 us
    transpose x1, other arithmetic, blend_ordered(): jnp.moveaxis(ordered.reshape(channels, count, rows * columns), 1, 0)  9.69 us
  transfers between devices with their start and end apart: 8, of which 6 were waited for; matrix products, arithmetic and copies ran while one was open for 5% of the time, Pallas kernels for 0%

commit v1 on v0

v1 whole, which is shorter than its diff:
```python
import functools

import jax
import jax.numpy as jnp
from jax import lax
from jax.experimental import pallas as pl
from jax.experimental.pallas import tpu as pltpu
from jax.sharding import Mesh
from jax.sharding import PartitionSpec as P

AXES = ("zh", "x", "c", "zl", "y")
CHUNKS = 4
ROW = 8
MESH = pl.DeviceIdType.MESH

AA_ORDER = [(dx, dz, dc) for dc in (0, 1) for dx, dz in
            ((1, 1), (3, 1), (0, 1), (2, 1), (1, 0), (3, 0), (2, 0), (0, 0))][:]
AA_ORDER = [p for p in AA_ORDER if p != (0, 0, 0)]
BA_ORDER = [(dy, dz) for dy in (2, 1, 3, 0) for dz in (1, 0) if (dy, dz) != (0, 0)]
XZ_ORDER = [(dx, dz) for dx, dz in
            ((2, 2), (1, 2), (3, 2), (2, 1), (2, 3), (1, 1), (3, 3), (1, 3), (3, 1),
             (0, 2), (2, 0), (1, 0), (0, 1), (3, 0), (0, 3))]

TIMES = {
    "prefix": (7, 7), "group": (12, 7), "trans": (16, 7), "scale": (37, 7), "sum_core": (40, 7),
    "sum_y": (49, 8), "sum_xz": (56, 8), "gather_y": (62, 9), "gather_core": (73, 10), "finish": (78, 10),
}


def kernel(tab, img, out, *scratch):
    ain, gin = scratch[:CHUNKS], scratch[CHUNKS:2 * CHUNKS]
    pre, gb, qb, qout, qin, tout, tin, col, cs, cin, a1, yin, a2, xin, send, recv, own = scratch[2 * CHUNKS:]
    zh, x, c, zl, y = (lax.axis_index(a) for a in AXES)
    z = zh * 2 + zl
    width = tin.shape[-1]
    tile = width // 8
    quarter = width // 4
    band = c * 8 + zh * 4 + x
    slot_b = y * 2 + zl

    def remote(src, dst, stage, k, device):
        cp = pltpu.make_async_remote_copy(
            src_ref=src, dst_ref=dst, send_sem=send.at[stage, k], recv_sem=recv.at[stage, k],
            device_id=device, device_id_type=MESH)
        cp.start()

    def arrived(ref, stage, k):
        pltpu.make_async_copy(ref, ref, recv.at[stage, k]).wait()

    def sent(ref, stage, k):
        pltpu.make_async_copy(ref, ref, send.at[stage, k]).wait()

    def aa_peers():
        for dx, dz, dc in AA_ORDER:
            xx, zz, cc = lax.rem(x + dx, 4), lax.rem(zh + dz, 2), lax.rem(c + dc, 2)
            yield cc * 8 + zz * 4 + xx, (zz, xx, cc, zl, y)

    def ba_peers():
        for dy, dz in BA_ORDER:
            yy, zz = lax.rem(y + dy, 4), lax.rem(zl + dz, 2)
            yield yy * 2 + zz, (zh, x, c, zz, yy)

    def xz_peers():
        for n, (dx, dz) in enumerate(XZ_ORDER):
            xx, zz = lax.rem(x + dx, 4), lax.rem(z + dz, 4)
            yield n, zz // 2 * 4 + xx, lax.rem(zz, 2), (zz // 2, xx, c, lax.rem(zz, 2), y)

    def y_peers():
        for n, dy in enumerate((2, 1, 3)):
            yy = lax.rem(y + dy, 4)
            yield n, yy, (zh, x, c, zl, yy)

    partner = (zh, x, 1 - c, zl, y)

    def cols(k):
        return pl.ds(k * width, width)

    def own_alpha(k):
        return pltpu.make_async_copy(img.at[3, band, :, cols(k)], ain[k].at[band], own.at[0, k])

    def own_color(k):
        return pltpu.make_async_copy(img.at[pl.ds(0, 3), :, :, cols(k)], col.at[k], own.at[1, k])

    def alpha(k):
        for r, device in aa_peers():
            remote(img.at[3, r, :, cols(k)], ain[k].at[band], 0, k, device)
        own_alpha(k).start()

    def prefix(k):
        own_alpha(k).wait()
        arrived(ain[k].at[pl.ds(0, 15)], 0, k)
        run = jnp.ones((ROW, width), jnp.float32)
        for m in range(16):
            pre[k, m] = run
            run = run * (1.0 - ain[k][tab[m]])
        for j in range(8):
            gb[k, j] = run[:, j * tile:(j + 1) * tile]
        gin[k][slot_b] = gb[k, slot_b]
        for j, device in ba_peers():
            remote(gb.at[k, j], gin[k].at[slot_b], 1, k, device)

    def group(k):
        arrived(gin[k].at[pl.ds(0, 7)], 1, k)
        run = jnp.ones((ROW, tile), jnp.float32)
        for m in range(8):
            qb[k, m] = run
            run = run * gin[k][tab[32 + m]]
        out[3, band, :, pl.ds(pl.multiple_of(k * width + slot_b * tile, 128), tile)] = 1.0 - run
        for j in range(8):
            qout[k, j] = qb[k, tab[40 + j]]
        qin[k, slot_b] = qout[k, slot_b]
        for j, device in ba_peers():
            remote(qout.at[k, j], qin.at[k, slot_b], 2, k, device)

    def trans(k):
        arrived(qin.at[k, pl.ds(0, 7)], 2, k)
        q = jnp.concatenate([qin[k, j] for j in range(8)], axis=1)
        for r in range(16):
            tout[k, r] = pre[k, tab[16 + r]] * q
        tin[k, band] = tout[k, band]
        for r, device in aa_peers():
            remote(tout.at[k, r], tin.at[k, band], 3, k, device)

    def scale(k):
        own_color(k).wait()
        arrived(tin.at[k, pl.ds(0, 15)], 3, k)

        def body(i, carry):
            r = (1 - c) * 8 + i
            t = tin[k, r]
            for ch in range(3):
                cs[k, ch, i] = col[k, ch, r] * t
            return carry

        lax.fori_loop(0, 8, body, 0)
        remote(cs.at[k], cin.at[k], 4, k, partner)

    def sum_core(k):
        arrived(cin.at[k], 4, k)

        def body(i, carry):
            r = c * 8 + i
            t = tin[k, r]
            for ch in range(3):
                a1[k, ch, i] = col[k, ch, r] * t + cin[k, ch, i]
            return carry

        lax.fori_loop(0, 8, body, 0)
        for n, yy, device in y_peers():
            at = pl.ds(pl.multiple_of(yy * quarter, 128), quarter)
            remote(a1.at[k, :, :, :, at], yin.at[k, n], 5, k, device)

    def sum_y(k):
        arrived(yin.at[k], 5, k)

        def body(i, carry):
            at = pl.ds(pl.multiple_of(y * quarter, 128), quarter)
            for ch in range(3):
                a2[k, ch, i] = a1[k, ch, i, :, at] + yin[k, 0, ch, i] + (yin[k, 1, ch, i] + yin[k, 2, ch, i])
            return carry

        lax.fori_loop(0, 8, body, 0)
        for n, r, t, device in xz_peers():
            at = pl.ds(pl.multiple_of(t * tile, 128), tile)
            remote(a2.at[k, :, r, :, at], xin.at[k, n], 6, k, device)

    def strip(k):
        return pl.ds(pl.multiple_of(k * width + slot_b * tile, 128), tile)

    def sum_xz(k):
        arrived(xin.at[k], 6, k)
        at = pl.ds(pl.multiple_of(zl * tile, 128), tile)
        for ch in range(3):
            s = a2[k, ch, zh * 4 + x, :, at]
            for n in range(15):
                s = s + xin[k, n, ch]
            out[ch, band, :, strip(k)] = s
        mine = out.at[:, band, :, strip(k)]
        for n, r, t, device in xz_peers():
            remote(mine, mine, 7, k, device)

    def piece(k, yy, cc):
        return out.at[:, pl.ds(pl.multiple_of(cc * 8, 8), 8), :, pl.ds(pl.multiple_of(k * width + yy * quarter, 128), quarter)]

    def gather_y(k):
        arrived(xin_like(k), 7, k)
        mine = piece(k, y, c)
        for n, yy, device in y_peers():
            remote(mine, mine, 8, k, device)
        remote(mine, mine, 9, k, partner)

    def xin_like(k):
        return out.at[:, pl.ds(0, 15), :, pl.ds(0, tile)]

    def gather_core(k):
        arrived(out.at[pl.ds(0, 3), pl.ds(0, 8), :, pl.ds(0, width)], 8, k)
        for n, yy, device in y_peers():
            mine = piece(k, yy, c)
            remote(mine, mine, 9, k, partner)

    def finish(k):
        arrived(out.at[:, pl.ds(0, 8), :, pl.ds(0, width)], 9, k)
        sent(ain[k].at[pl.ds(0, 15)], 0, k)
        sent(gb.at[k, pl.ds(0, 7)], 1, k)
        sent(qout.at[k, pl.ds(0, 7)], 2, k)
        sent(tout.at[k, pl.ds(0, 15)], 3, k)
        sent(cs.at[k], 4, k)
        sent(yin.at[k], 5, k)
        sent(xin.at[k], 6, k)
        sent(xin_like(k), 7, k)
        sent(out.at[pl.ds(0, 3), pl.ds(0, 8), :, pl.ds(0, width)], 8, k)
        sent(out.at[:, pl.ds(0, 8), :, pl.ds(0, width)], 9, k)

    stages = dict(prefix=prefix, group=group, trans=trans, scale=scale, sum_core=sum_core, sum_y=sum_y,
                  sum_xz=sum_xz, gather_y=gather_y, gather_core=gather_core, finish=finish)
    for k in range(CHUNKS):
        alpha(k)
    for k in range(CHUNKS):
        own_color(k).start()
    names = list(stages)
    plan = sorted((TIMES[s][0] + TIMES[s][1] * k, names.index(s), k) for s in names for k in range(CHUNKS))
    for when, s, k in plan:
        stages[names[s]](k)


def tables(depth, brick_map):
    count = depth.shape[0]
    bricks = jnp.arange(count, dtype=jnp.int32)
    rank = jnp.sum(jnp.where(brick_map[:, None] == bricks[None, :], depth[None, :], 0), axis=1)
    rank = rank.reshape(2, 4, 2, 2, 4)
    group = rank[0, 0, 0] // 16
    group = group.T.reshape(8)
    zl, y = lax.axis_index("zl"), lax.axis_index("y")
    inner = lax.dynamic_slice(rank, (0, 0, 0, zl, y), (2, 4, 2, 1, 1)).reshape(2, 4, 2) % 16
    inner = inner.transpose(2, 0, 1).reshape(16)

    def inverse(r, n):
        i = jnp.arange(n, dtype=jnp.int32)
        return jnp.sum(jnp.where(r[None, :] == i[:, None], i[None, :], 0), axis=1)

    return jnp.concatenate([inverse(inner, 16), inner, inverse(group, 8), group]).astype(jnp.int32)


def local(images, depth, brick_map):
    channels, rows, columns = images.shape[1:]
    tab = tables(depth, brick_map)
    width = columns // CHUNKS
    tile, quarter = width // 8, width // 4
    f = jnp.float32
    n = CHUNKS
    vm = lambda *s: pltpu.VMEM(s, f)
    out = pl.pallas_call(
        kernel,
        out_shape=jax.ShapeDtypeStruct((channels, rows // ROW, ROW, columns), f),
        in_specs=[pl.BlockSpec(memory_space=pltpu.SMEM), pl.BlockSpec(memory_space=pl.ANY)],
        out_specs=pl.BlockSpec(memory_space=pltpu.VMEM),
        scratch_shapes=[
            *[vm(16, ROW, width)] * n, *[vm(8, ROW, tile)] * n,
            vm(n, 16, ROW, width), vm(n, 8, ROW, tile), vm(n, 8, ROW, tile), vm(n, 8, ROW, tile), vm(n, 8, ROW, tile),
            vm(n, 16, ROW, width), vm(n, 16, ROW, width),
            vm(n, 3, 16, ROW, width), vm(n, 3, 8, ROW, width), vm(n, 3, 8, ROW, width), vm(n, 3, 8, ROW, width),
            vm(n, 3, 3, 8, ROW, quarter), vm(n, 3, 8, ROW, quarter), vm(n, 15, 3, ROW, tile),
            pltpu.SemaphoreType.DMA((10, n)), pltpu.SemaphoreType.DMA((10, n)), pltpu.SemaphoreType.DMA((2, n)),
        ],
        compiler_params=pltpu.CompilerParams(has_side_effects=True, vmem_limit_bytes=60 * 2**20),
    )(tab, images.reshape(channels, rows // ROW, ROW, columns))
    return out.reshape(channels, rows, columns)


def solution(mesh):
    torus = Mesh(mesh.devices.reshape(2, 4, 2, 2, 4), AXES)
    return jax.shard_map(
        local,
        mesh=torus,
        in_specs=(P(("zh", "x", "c", "zl", "y"), None, None, None), P(), P()),
        out_specs=P(),
        check_vma=False,
    )
```

time: 427 us -> 163 us (0.38)
  waiting for transfers between devices: 199 us -> 0 us
  Pallas kernels: 0 us -> 150 us
  blocking collectives: 106 us -> 0 us
  local copies, waits for them, and re-layouts: 65.4 us -> 8.36 us
  other arithmetic: 27.9 us -> 1.7 us
  starting transfers between devices: 14.3 us -> 0 us
  between operations: 13.8 us -> 0.04 us
    pallas_call x0 -> x1, Pallas kernels: none -> 150 us  [local(): pl.pallas_call(kernel, out_shape=jax.ShapeDtypeStruct((channels, rows //...]
    all_to_all x2 -> x0, waiting for transfers between devices: 120 us -> none  [the longest x1 110 us: local(): lax.all_to_all(bands, AA, split_axis=1, concat_axis=1, tiled=True)]
    all_gather x14 -> x0, blocking collectives: 106 us -> none  [gather_in_order(): pieces = lax.all_gather(pieces, axes[k])]
    all_gather x6 -> x0, waiting for transfers between devices: 77.7 us -> none  [gather_in_order(): pieces = lax.all_gather(pieces, axes[k])]
    gather x3 -> x0, local copies, waits for them, and re-layouts: 19.6 us -> none  [blend_ordered(): ordered = jnp.take(stacked, ordering, axis=1)]
    transpose x2, other arithmetic: 18.8 us -> 0.02 us  [the longest x1 0.01 us: tables(): inner = inner.transpose(2, 0, 1).reshape(16)]
    all_gather x11 -> x0, local copies, waits for them, and re-layouts: 18.5 us -> none  [gather_in_order(): pieces = lax.all_gather(pieces, axes[k])]
    all_to_all x2 -> x0, starting transfers between devices: 13.9 us -> none  [the longest x1 9.25 us: local(): lax.all_to_all(bands, AA, split_axis=1, concat_axis=1, tiled=True)]
  transfers between devices with their start and end apart: 8 -> 0, of which waited for: 6 -> 0; matrix products, arithmetic and copies ran while one was open for 5% -> 0% of each run, Pallas kernels for 0% -> 0%
where the time goes in v1:
time: 163 us; the launch traced here: 160 us
  Pallas kernels  150 us (92%)
  local copies, waits for them, and re-layouts  8.36 us (5%)
  other arithmetic  1.7 us (1%)
    pallas_call x1, Pallas kernels, local(): pl.pallas_call(kernel, out_shape=jax.ShapeDtypeStruct((channels, rows //...  150 us
    unnamed x1, local copies, waits for them, and re-layouts  7.77 us

profile of v1, /device:TPU:1, one launch (start us, length us, event | category | flops | bytes accessed | tf_op | source)
XLA Modules:
  0.0 160.0 jit_solution(18367562363410502166)
XLA Ops:
  0.0 0.8 select_reduce_fusion
  0.8 0.1 reshape.18
  1.0 0.1 constant_dynamic-slice_fusion
  1.1 0.1 copy.10
  1.2 0.1 eq.48
  1.3 0.1 select_reduce_fusion.1
  1.4 0.1 copy.12
  1.5 0.1 eq.52
  1.6 0.1 select_reduce_fusion.2
  1.7 0.6 pad_add_fusion.tab
  2.3 149.9 %shard_map.37 = f32[4,16,8,4096]{3,2,1,0:T(8,128)} custom-call(s32[48]{0:T(128)} %pad_add_fusion.tab, f32[4,16,8,4096]{3,2,1,0:T(8,128)} %bitcast.15), custom_call_target="tpu_custom_call" | custom-call | tf_op jit(solution)/shard_map/pallas_call | solution.py:252
  152.2 7.8 %copy.14 = f32[4,128,4096]{2,1,0:T(8,128)} copy(f32[4,128,4096]{2,1,0:T(8,128)} %bitcast.14) | data formatting | bytes 16777216
  (3 shorter events, 0.0 us)

commit v2 on v1

--- a/solution.py
+++ b/solution.py
@@ -21,15 +21,19 @@
             ((2, 2), (1, 2), (3, 2), (2, 1), (2, 3), (1, 1), (3, 3), (1, 3), (3, 1),
              (0, 2), (2, 0), (1, 0), (0, 1), (3, 0), (0, 3))]
 
-TIMES = {
-    "prefix": (7, 7), "group": (12, 7), "trans": (16, 7), "scale": (37, 7), "sum_core": (40, 7),
-    "sum_y": (49, 8), "sum_xz": (56, 8), "gather_y": (62, 9), "gather_core": (73, 10), "finish": (78, 10),
-}
-
-
-def kernel(tab, img, out, *scratch):
+PLAN = (
+    "alpha0", "alpha1", "load", "prefix0", "alpha2", "group0", "prefix1", "alpha3", "trans0", "group1",
+    "prefix2", "trans1", "group2", "prefix3", "trans2", "scale0", "sum_core0", "group3", "trans3", "around0",
+    "scale1", "sum_core1", "sum_y0", "around1", "sum_xz0", "gather_y0", "sum_y1", "scale2", "sum_core2",
+    "forward0", "sum_xz1", "around2", "gather_core0", "gather_y1", "scale3", "sum_core3", "sum_y2",
+    "forward1", "around3", "sum_xz2", "gather_core1", "gather_y2", "sum_y3", "sum_xz3", "forward2",
+    "gather_y3", "gather_core2", "forward3", "gather_core3", "finish",
+)
+
+
+def kernel(depth, bricks, img, out, *scratch):
     ain, gin = scratch[:CHUNKS], scratch[CHUNKS:2 * CHUNKS]
-    pre, gb, qb, qout, qin, tout, tin, col, cs, cin, a1, yin, a2, xin, send, recv, own = scratch[2 * CHUNKS:]
+    pre, gb, qb, qout, qin, tout, tin, col, cs, cin, a1, ys, b1, yin, a2, xin, send, recv, own = scratch[2 * CHUNKS:]
     zh, x, c, zl, y = (lax.axis_index(a) for a in AXES)
     z = zh * 2 + zl
     width = tin.shape[-1]
@@ -65,12 +69,32 @@
             xx, zz = lax.rem(x + dx, 4), lax.rem(z + dz, 4)
             yield n, zz // 2 * 4 + xx, lax.rem(zz, 2), (zz // 2, xx, c, lax.rem(zz, 2), y)
 
-    def y_peers():
-        for n, dy in enumerate((2, 1, 3)):
-            yy = lax.rem(y + dy, 4)
-            yield n, yy, (zh, x, c, zl, yy)
-
     partner = (zh, x, 1 - c, zl, y)
+
+    up = (zh, x, c, zl, lax.rem(y + 1, 4))
+    down = (zh, x, c, zl, lax.rem(y + 3, 4))
+
+    def meet():
+        barrier = pltpu.get_barrier_semaphore()
+        devices = [d for _, d in aa_peers()] + [d for _, d in ba_peers()]
+        devices += [(zz // 2, xx, c, lax.rem(zz, 2), y) for xx, zz in
+                    ((lax.rem(x + dx, 4), lax.rem(z + dz, 4)) for dx in range(4) for dz in (1, 3))]
+        for device in devices:
+            pl.semaphore_signal(barrier, inc=1, device_id=device, device_id_type=MESH)
+        pl.semaphore_wait(barrier, len(devices))
+
+    def tables():
+        def rank_of(zz, xx, cc, zzl, yy):
+            return depth[bricks[(((zz * 4 + xx) * 2 + cc) * 2 + zzl) * 4 + yy]]
+
+        inner = [lax.rem(rank_of(r // 4 % 2, r % 4, r // 8, zl, y), 16) for r in range(16)]
+        group = [lax.div(rank_of(zh, x, c, j % 2, j // 2), 16) for j in range(8)]
+
+        def inverse(ranks, m):
+            return functools.reduce(lambda a, iv: jnp.where(iv[1] == m, iv[0], a), enumerate(ranks), 0)
+
+        return ([inverse(inner, m) for m in range(16)] + inner
+                + [inverse(group, m) for m in range(8)] + group)
 
     def cols(k):
         return pl.ds(k * width, width)
@@ -146,17 +170,31 @@
             return carry
 
         lax.fori_loop(0, 8, body, 0)
-        for n, yy, device in y_peers():
-            at = pl.ds(pl.multiple_of(yy * quarter, 128), quarter)
-            remote(a1.at[k, :, :, :, at], yin.at[k, n], 5, k, device)
+        def part(dy, half):
+            q = pl.ds(pl.multiple_of(lax.rem(y + dy, 4) * quarter, 128), quarter)
+            return a1.at[k, :, 4 * half:4 * half + 4, :, q]
+
+        remote(part(2, 0), ys.at[k, 0], 5, k, up)
+        remote(part(2, 1), ys.at[k, 1], 5, k, down)
+        remote(part(1, 1), yin.at[k, 0, :, 4:8], 10, k, up)
+        remote(part(3, 0), yin.at[k, 1, :, 0:4], 10, k, down)
+
+    def around(k):
+        arrived(ys.at[k], 5, k)
+        for n, dy, device in ((0, 1, up), (1, 3, down)):
+            q = pl.ds(pl.multiple_of(lax.rem(y + dy, 4) * quarter, 128), quarter)
+            for ch in range(3):
+                for i in range(4):
+                    b1[k, n, ch, i] = a1[k, ch, 4 * n + i, :, q] + ys[k, n, ch, i]
+            remote(b1.at[k, n], yin.at[k, n, :, 4 * n:4 * n + 4], 10, k, device)
 
     def sum_y(k):
-        arrived(yin.at[k], 5, k)
+        arrived(yin.at[k], 10, k)
 
         def body(i, carry):
             at = pl.ds(pl.multiple_of(y * quarter, 128), quarter)
             for ch in range(3):
-                a2[k, ch, i] = a1[k, ch, i, :, at] + yin[k, 0, ch, i] + (yin[k, 1, ch, i] + yin[k, 2, ch, i])
+                a2[k, ch, i] = a1[k, ch, i, :, at] + (yin[k, 0, ch, i] + yin[k, 1, ch, i])
             return carry
 
         lax.fori_loop(0, 8, body, 0)
@@ -185,65 +223,68 @@
     def gather_y(k):
         arrived(xin_like(k), 7, k)
         mine = piece(k, y, c)
-        for n, yy, device in y_peers():
-            remote(mine, mine, 8, k, device)
+        remote(mine, mine, 8, k, up)
+        remote(mine, mine, 11, k, down)
         remote(mine, mine, 9, k, partner)
+
+    def forward(k):
+        whole = out.at[:, pl.ds(0, 8), :, pl.ds(0, quarter)]
+        arrived(whole, 8, k)
+        below = piece(k, lax.rem(y + 3, 4), c)
+        remote(below.at[pl.ds(0, 2)], below.at[pl.ds(0, 2)], 12, k, up)
+        remote(below, below, 9, k, partner)
+        arrived(whole, 11, k)
+        above = piece(k, lax.rem(y + 1, 4), c)
+        remote(above.at[pl.ds(2, 2)], above.at[pl.ds(2, 2)], 12, k, down)
+        remote(above, above, 9, k, partner)
 
     def xin_like(k):
         return out.at[:, pl.ds(0, 15), :, pl.ds(0, tile)]
 
     def gather_core(k):
-        arrived(out.at[pl.ds(0, 3), pl.ds(0, 8), :, pl.ds(0, width)], 8, k)
-        for n, yy, device in y_peers():
-            mine = piece(k, yy, c)
-            remote(mine, mine, 9, k, partner)
-
-    def finish(k):
-        arrived(out.at[:, pl.ds(0, 8), :, pl.ds(0, width)], 9, k)
-        sent(ain[k].at[pl.ds(0, 15)], 0, k)
-        sent(gb.at[k, pl.ds(0, 7)], 1, k)
-        sent(qout.at[k, pl.ds(0, 7)], 2, k)
-        sent(tout.at[k, pl.ds(0, 15)], 3, k)
-        sent(cs.at[k], 4, k)
-        sent(yin.at[k], 5, k)
-        sent(xin.at[k], 6, k)
-        sent(xin_like(k), 7, k)
-        sent(out.at[pl.ds(0, 3), pl.ds(0, 8), :, pl.ds(0, width)], 8, k)
-        sent(out.at[:, pl.ds(0, 8), :, pl.ds(0, width)], 9, k)
-
-    stages = dict(prefix=prefix, group=group, trans=trans, scale=scale, sum_core=sum_core, sum_y=sum_y,
-                  sum_xz=sum_xz, gather_y=gather_y, gather_core=gather_core, finish=finish)
-    for k in range(CHUNKS):
-        alpha(k)
-    for k in range(CHUNKS):
-        own_color(k).start()
-    names = list(stages)
-    plan = sorted((TIMES[s][0] + TIMES[s][1] * k, names.index(s), k) for s in names for k in range(CHUNKS))
-    for when, s, k in plan:
-        stages[names[s]](k)
-
-
-def tables(depth, brick_map):
-    count = depth.shape[0]
-    bricks = jnp.arange(count, dtype=jnp.int32)
-    rank = jnp.sum(jnp.where(brick_map[:, None] == bricks[None, :], depth[None, :], 0), axis=1)
-    rank = rank.reshape(2, 4, 2, 2, 4)
-    group = rank[0, 0, 0] // 16
-    group = group.T.reshape(8)
-    zl, y = lax.axis_index("zl"), lax.axis_index("y")
-    inner = lax.dynamic_slice(rank, (0, 0, 0, zl, y), (2, 4, 2, 1, 1)).reshape(2, 4, 2) % 16
-    inner = inner.transpose(2, 0, 1).reshape(16)
-
-    def inverse(r, n):
-        i = jnp.arange(n, dtype=jnp.int32)
-        return jnp.sum(jnp.where(r[None, :] == i[:, None], i[None, :], 0), axis=1)
-
-    return jnp.concatenate([inverse(inner, 16), inner, inverse(group, 8), group]).astype(jnp.int32)
+        arrived(out.at[:, pl.ds(0, 8), :, pl.ds(0, quarter)], 12, k)
+        far = piece(k, lax.rem(y + 2, 4), c)
+        remote(far, far, 9, k, partner)
+
+    def finish():
+        whole = out.at[:, pl.ds(0, 8), :, pl.ds(0, quarter)]
+        for k in range(CHUNKS):
+            sent(ain[k].at[pl.ds(0, 15)], 0, k)
+            sent(gb.at[k, pl.ds(0, 7)], 1, k)
+            sent(qout.at[k, pl.ds(0, 7)], 2, k)
+            sent(tout.at[k, pl.ds(0, 15)], 3, k)
+            sent(cs.at[k], 4, k)
+            sent(ys.at[k], 5, k)
+            sent(yin.at[k], 10, k)
+            sent(xin.at[k], 6, k)
+            sent(xin_like(k), 7, k)
+            sent(whole, 8, k)
+            sent(whole, 11, k)
+            sent(whole, 12, k)
+            arrived(out.at[:, pl.ds(0, 8), :, pl.ds(0, width)], 9, k)
+            sent(out.at[:, pl.ds(0, 8), :, pl.ds(0, width)], 9, k)
+
+    def load():
+        for k in range(CHUNKS):
+            own_color(k).start()
+        tab.extend(tables())
+
+    tab = []
+    stages = dict(alpha=alpha, prefix=prefix, group=group, trans=trans, scale=scale, sum_core=sum_core, around=around, sum_y=sum_y,
+                  sum_xz=sum_xz, gather_y=gather_y, forward=forward, gather_core=gather_core)
+    meet()
+    for name in PLAN:
+        with jax.named_scope(name):
+            if name == "load":
+                load()
+            elif name == "finish":
+                finish()
+            else:
+                stages[name[:-1]](int(name[-1]))
 
 
 def local(images, depth, brick_map):
     channels, rows, columns = images.shape[1:]
-    tab = tables(depth, brick_map)
     width = columns // CHUNKS
     tile, quarter = width // 8, width // 4
     f = jnp.float32
@@ -251,19 +292,19 @@
     vm = lambda *s: pltpu.VMEM(s, f)
     out = pl.pallas_call(
         kernel,
-        out_shape=jax.ShapeDtypeStruct((channels, rows // ROW, ROW, columns), f),
-        in_specs=[pl.BlockSpec(memory_space=pltpu.SMEM), pl.BlockSpec(memory_space=pl.ANY)],
+        out_shape=pltpu.VMEM((channels, rows // ROW, ROW, columns), f),
+        in_specs=[pl.BlockSpec(memory_space=pltpu.SMEM), pl.BlockSpec(memory_space=pltpu.SMEM), pl.BlockSpec(memory_space=pl.ANY)],
         out_specs=pl.BlockSpec(memory_space=pltpu.VMEM),
         scratch_shapes=[
             *[vm(16, ROW, width)] * n, *[vm(8, ROW, tile)] * n,
             vm(n, 16, ROW, width), vm(n, 8, ROW, tile), vm(n, 8, ROW, tile), vm(n, 8, ROW, tile), vm(n, 8, ROW, tile),
             vm(n, 16, ROW, width), vm(n, 16, ROW, width),
             vm(n, 3, 16, ROW, width), vm(n, 3, 8, ROW, width), vm(n, 3, 8, ROW, width), vm(n, 3, 8, ROW, width),
-            vm(n, 3, 3, 8, ROW, quarter), vm(n, 3, 8, ROW, quarter), vm(n, 15, 3, ROW, tile),
-            pltpu.SemaphoreType.DMA((10, n)), pltpu.SemaphoreType.DMA((10, n)), pltpu.SemaphoreType.DMA((2, n)),
+            vm(n, 2, 3, 4, ROW, quarter), vm(n, 2, 3, 4, ROW, quarter), vm(n, 2, 3, 8, ROW, quarter), vm(n, 3, 8, ROW, quarter), vm(n, 15, 3, ROW, tile),
+            pltpu.SemaphoreType.DMA((13, n)), pltpu.SemaphoreType.DMA((13, n)), pltpu.SemaphoreType.DMA((2, n)),
         ],
-        compiler_params=pltpu.CompilerParams(has_side_effects=True, vmem_limit_bytes=60 * 2**20),
-    )(tab, images.reshape(channels, rows // ROW, ROW, columns))
+        compiler_params=pltpu.CompilerParams(has_side_effects=True, collective_id=0, vmem_limit_bytes=48 * 2**20),
+    )(depth, brick_map, images.reshape(channels, rows // ROW, ROW, columns))
     return out.reshape(channels, rows, columns)
 
 

time: 163 us -> 135 us (0.83); the launches traced: 160 us -> 135 us
  Pallas kernels: 150 us -> 131 us
  local copies, waits for them, and re-layouts: 8.36 us -> 3.4 us
  other arithmetic: 1.7 us -> 0 us
    pallas_call x1, Pallas kernels: 150 us -> 131 us  [local(): pl.pallas_call(kernel, out_shape=pltpu.VMEM((channels, rows // ROW, ROW,...]
    unnamed x1, local copies, waits for them, and re-layouts: 7.77 us -> 3.4 us
where the time goes in v2:
time: 135 us
  Pallas kernels  131 us (97%)
  local copies, waits for them, and re-layouts  3.4 us (3%)
    pallas_call x1, Pallas kernels, local(): pl.pallas_call(kernel, out_shape=pltpu.VMEM((channels, rows // ROW, ROW,...  131 us
    unnamed x1, local copies, waits for them, and re-layouts  3.4 us

profile of v2, /device:TPU:1, one launch (start us, length us, event | category | flops | bytes accessed | tf_op | source)
XLA Modules:
  0.0 134.6 jit_solution(3526326332521261388)
XLA Ops:
  0.0 131.2 %shard_map.37 = f32[4,16,8,4096]{3,2,1,0:T(8,128)S(1)} custom-call(s32[128]{0:T(128)} %depth.1, s32[128]{0:T(128)} %bricks.1, f32[4,16,8,4096]{3,2,1,0:T(8,128)} %bitcast.3), custom_call_target="tpu_custom_call" | custom-call | tf_op jit(solution)/shard_map/pallas_call | solution.py:293
  131.2 3.4 %copy.5 = f32[4,128,4096]{2,1,0:T(8,128)} copy(f32[4,128,4096]{2,1,0:T(8,128)S(1)} %bitcast.2) | data formatting | bytes 16777216

commit v3 on v2

--- a/solution.py
+++ b/solution.py
@@ -22,12 +22,12 @@
              (0, 2), (2, 0), (1, 0), (0, 1), (3, 0), (0, 3))]
 
 PLAN = (
-    "alpha0", "alpha1", "load", "prefix0", "alpha2", "group0", "prefix1", "alpha3", "trans0", "group1",
-    "prefix2", "trans1", "group2", "prefix3", "trans2", "scale0", "sum_core0", "group3", "trans3", "around0",
-    "scale1", "sum_core1", "sum_y0", "around1", "sum_xz0", "gather_y0", "sum_y1", "scale2", "sum_core2",
-    "forward0", "sum_xz1", "around2", "gather_core0", "gather_y1", "scale3", "sum_core3", "sum_y2",
-    "forward1", "around3", "sum_xz2", "gather_core1", "gather_y2", "sum_y3", "sum_xz3", "forward2",
-    "gather_y3", "gather_core2", "forward3", "gather_core3", "finish",
+    "alpha0", "alpha1", "load", "prefix0", "alpha3", "prefix1", "group0", "alpha2", "prefix3", "group1",
+    "trans0", "prefix2", "group3", "trans1", "scale0", "group2", "sum_core0", "trans3", "scale1", "around0",
+    "sum_core1", "trans2", "scale3", "sum_y0", "around1", "sum_core3", "scale2", "sum_y1", "around3",
+    "sum_core2", "sum_xz0", "sum_y3", "sum_xz1", "around2", "gather_y0", "sum_xz3", "sum_y2", "gather_y1",
+    "gather_y3", "forward1", "forward0", "sum_xz2", "gather_y2", "gather_core1", "forward3", "forward2",
+    "gather_core0", "gather_core3", "gather_core2", "finish",
 )
 
 
@@ -105,10 +105,11 @@
     def own_color(k):
         return pltpu.make_async_copy(img.at[pl.ds(0, 3), :, :, cols(k)], col.at[k], own.at[1, k])
 
-    def alpha(k):
-        for r, device in aa_peers():
+    def alpha(k, begin=0, end=15):
+        for r, device in list(aa_peers())[begin:end]:
             remote(img.at[3, r, :, cols(k)], ain[k].at[band], 0, k, device)
-        own_alpha(k).start()
+        if begin == 0:
+            own_alpha(k).start()
 
     def prefix(k):
         own_alpha(k).wait()
@@ -279,6 +280,10 @@
                 load()
             elif name == "finish":
                 finish()
+            elif name[-1] == "a":
+                alpha(int(name[-2]), 0, 7)
+            elif name[-1] == "b":
+                alpha(int(name[-2]), 7, 15)
             else:
                 stages[name[:-1]](int(name[-1]))
 

time: 135 us -> 116 us (0.86)
  Pallas kernels: 131 us -> 112 us
    pallas_call x1, Pallas kernels: 131 us -> 112 us  [local(): pl.pallas_call(kernel, out_shape=pltpu.VMEM((channels, rows // ROW, ROW,...]
where the time goes in v3:
time: 116 us; the launch traced here: 115 us
  Pallas kernels  112 us (97%)
  local copies, waits for them, and re-layouts  3.4 us (3%)
    pallas_call x1, Pallas kernels, local(): pl.pallas_call(kernel, out_shape=pltpu.VMEM((channels, rows // ROW, ROW,...  112 us
    unnamed x1, local copies, waits for them, and re-layouts  3.4 us

profile of v3, /device:TPU:1, one launch (start us, length us, event | category | flops | bytes accessed | tf_op | source)
XLA Modules:
  0.0 115.4 jit_solution(12279937585243335258)
XLA Ops:
  0.0 112.0 %shard_map.37 = f32[4,16,8,4096]{3,2,1,0:T(8,128)S(1)} custom-call(s32[128]{0:T(128)} %depth.1, s32[128]{0:T(128)} %bricks.1, f32[4,16,8,4096]{3,2,1,0:T(8,128)} %bitcast.3), custom_call_target="tpu_custom_call" | custom-call | tf_op jit(solution)/shard_map/pallas_call | solution.py:298
  112.0 3.4 %copy.5 = f32[4,128,4096]{2,1,0:T(8,128)} copy(f32[4,128,4096]{2,1,0:T(8,128)S(1)} %bitcast.2) | data formatting | bytes 16777216

commit v4 on v3

--- a/solution.py
+++ b/solution.py
@@ -10,6 +10,7 @@
 
 AXES = ("zh", "x", "c", "zl", "y")
 CHUNKS = 4
+SHARE = (4, 3, 2, 2)
 ROW = 8
 MESH = pl.DeviceIdType.MESH
 
@@ -22,12 +23,13 @@
              (0, 2), (2, 0), (1, 0), (0, 1), (3, 0), (0, 3))]
 
 PLAN = (
-    "alpha0", "alpha1", "load", "prefix0", "alpha3", "prefix1", "group0", "alpha2", "prefix3", "group1",
-    "trans0", "prefix2", "group3", "trans1", "scale0", "group2", "sum_core0", "trans3", "scale1", "around0",
-    "sum_core1", "trans2", "scale3", "sum_y0", "around1", "sum_core3", "scale2", "sum_y1", "around3",
-    "sum_core2", "sum_xz0", "sum_y3", "sum_xz1", "around2", "gather_y0", "sum_xz3", "sum_y2", "gather_y1",
-    "gather_y3", "forward1", "forward0", "sum_xz2", "gather_y2", "gather_core1", "forward3", "forward2",
-    "gather_core0", "gather_core3", "gather_core2", "finish",
+    "alpha0", "load", "alpha1", "prefix0", "alpha2", "group0", "prefix1", "alpha3", "group1", "prefix2",
+    "trans0", "prefix3", "group2", "trans1", "scale0", "group3", "sum_core0", "trans2", "scale1", "around0",
+    "sum_core1", "trans3", "scale2", "around1", "sum_core2", "sum_y1", "sum_y0", "scale3", "around2",
+    "sum_core3", "sum_xz1", "sum_y2", "sum_xz0", "around3", "gather_y1", "sum_y3", "sum_xz2", "gather_y0",
+    "spread1", "sum_xz3", "gather_y2", "spread2", "forward1", "gather_y3", "forward2", "spread3",
+    "gather_core1", "spread_core1", "spread_core2", "forward0", "gather_core2", "forward3", "gather_core0",
+    "spread_core3", "gather_core3", "finish",
 )
 
 
@@ -38,9 +40,9 @@
     z = zh * 2 + zl
     width = tin.shape[-1]
     tile = width // 8
-    quarter = width // 4
+    half = width // 2
     band = c * 8 + zh * 4 + x
-    slot_b = y * 2 + zl
+    slot_b = zl * 4 + y
 
     def remote(src, dst, stage, k, device):
         cp = pltpu.make_async_remote_copy(
@@ -62,7 +64,7 @@
     def ba_peers():
         for dy, dz in BA_ORDER:
             yy, zz = lax.rem(y + dy, 4), lax.rem(zl + dz, 2)
-            yield yy * 2 + zz, (zh, x, c, zz, yy)
+            yield zz * 4 + yy, (zh, x, c, zz, yy)
 
     def xz_peers():
         for n, (dx, dz) in enumerate(XZ_ORDER):
@@ -88,7 +90,7 @@
             return depth[bricks[(((zz * 4 + xx) * 2 + cc) * 2 + zzl) * 4 + yy]]
 
         inner = [lax.rem(rank_of(r // 4 % 2, r % 4, r // 8, zl, y), 16) for r in range(16)]
-        group = [lax.div(rank_of(zh, x, c, j % 2, j // 2), 16) for j in range(8)]
+        group = [lax.div(rank_of(zh, x, c, j // 4, j % 4), 16) for j in range(8)]
 
         def inverse(ranks, m):
             return functools.reduce(lambda a, iv: jnp.where(iv[1] == m, iv[0], a), enumerate(ranks), 0)
@@ -167,88 +169,105 @@
             r = c * 8 + i
             t = tin[k, r]
             for ch in range(3):
-                a1[k, ch, i] = col[k, ch, r] * t + cin[k, ch, i]
+                v = col[k, ch, r] * t + cin[k, ch, i]
+                a1[k, ch, i, 0] = v[:, :half]
+                a1[k, ch, i, 1] = v[:, half:]
             return carry
 
         lax.fori_loop(0, 8, body, 0)
-        def part(dy, half):
-            q = pl.ds(pl.multiple_of(lax.rem(y + dy, 4) * quarter, 128), quarter)
-            return a1.at[k, :, 4 * half:4 * half + 4, :, q]
+        def part(dy, h):
+            return a1.at[k, :, 4 * h:4 * h + 4, :, :, tiles(dy)]
 
         remote(part(2, 0), ys.at[k, 0], 5, k, up)
         remote(part(2, 1), ys.at[k, 1], 5, k, down)
         remote(part(1, 1), yin.at[k, 0, :, 4:8], 10, k, up)
         remote(part(3, 0), yin.at[k, 1, :, 0:4], 10, k, down)
 
+    def tiles(dy):
+        return pl.ds(pl.multiple_of(lax.rem(y + dy, 4) * tile, 128), tile)
+
     def around(k):
         arrived(ys.at[k], 5, k)
         for n, dy, device in ((0, 1, up), (1, 3, down)):
-            q = pl.ds(pl.multiple_of(lax.rem(y + dy, 4) * quarter, 128), quarter)
             for ch in range(3):
                 for i in range(4):
-                    b1[k, n, ch, i] = a1[k, ch, 4 * n + i, :, q] + ys[k, n, ch, i]
+                    b1[k, n, ch, i] = a1[k, ch, 4 * n + i, :, :, tiles(dy)] + ys[k, n, ch, i]
             remote(b1.at[k, n], yin.at[k, n, :, 4 * n:4 * n + 4], 10, k, device)
 
     def sum_y(k):
         arrived(yin.at[k], 10, k)
 
         def body(i, carry):
-            at = pl.ds(pl.multiple_of(y * quarter, 128), quarter)
             for ch in range(3):
-                a2[k, ch, i] = a1[k, ch, i, :, at] + (yin[k, 0, ch, i] + yin[k, 1, ch, i])
+                a2[k, ch, i] = a1[k, ch, i, :, :, tiles(0)] + (yin[k, 0, ch, i] + yin[k, 1, ch, i])
             return carry
 
         lax.fori_loop(0, 8, body, 0)
         for n, r, t, device in xz_peers():
-            at = pl.ds(pl.multiple_of(t * tile, 128), tile)
-            remote(a2.at[k, :, r, :, at], xin.at[k, n], 6, k, device)
+            remote(a2.at[k, :, r, t], xin.at[k, n], 6, k, device)
 
     def strip(k):
         return pl.ds(pl.multiple_of(k * width + slot_b * tile, 128), tile)
 
     def sum_xz(k):
         arrived(xin.at[k], 6, k)
-        at = pl.ds(pl.multiple_of(zl * tile, 128), tile)
         for ch in range(3):
-            s = a2[k, ch, zh * 4 + x, :, at]
+            v = a2[k, ch, zh * 4 + x, zl]
             for n in range(15):
-                s = s + xin[k, n, ch]
-            out[ch, band, :, strip(k)] = s
-        mine = out.at[:, band, :, strip(k)]
+                v = v + xin[k, n, ch]
+            out[ch, band, :, strip(k)] = v
+        if SHARE[k] < 4:
+            mine = out.at[SHARE[k]:4, band, :, strip(k)]
+            for dy in (2, 1, 3):
+                remote(mine, mine, 13, k, (zh, x, c, zl, lax.rem(y + dy, 4)))
+        if SHARE[k] > 0:
+            mine = out.at[0:SHARE[k], band, :, strip(k)]
+            for n, r, t, device in xz_peers():
+                remote(mine, mine, 7, k, device)
+
+    def block(k, first, last, count, columns):
+        return out.at[first:last, pl.ds(0, count), :, pl.ds(0, columns)]
+
+    def piece(k, dy, h):
+        at = pl.multiple_of(k * width + h * half + lax.rem(y + dy, 4) * tile, 128)
+        return out.at[0:SHARE[k], pl.ds(pl.multiple_of(c * 8, 8), 8), :, pl.ds(at, tile)]
+
+    def gather_y(k):
+        arrived(block(k, 0, SHARE[k], 15, tile), 7, k)
+        for h in range(2):
+            mine = piece(k, 0, h)
+            remote(mine, mine, 8, k, up)
+            remote(mine, mine, 11, k, down)
+            remote(mine, mine, 9, k, partner)
+
+    def forward(k):
+        arrived(block(k, 0, SHARE[k], 8, 2 * tile), 8, k)
+        below = [piece(k, 3, h) for h in range(2)]
+        remote(below[0], below[0], 12, k, up)
+        arrived(block(k, 0, SHARE[k], 8, 2 * tile), 11, k)
+        above = [piece(k, 1, h) for h in range(2)]
+        remote(above[1], above[1], 12, k, down)
+        for ref in below + above:
+            remote(ref, ref, 9, k, partner)
+
+    def gather_core(k):
+        arrived(block(k, 0, SHARE[k], 8, 2 * tile), 12, k)
+        for h in range(2):
+            far = piece(k, 2, h)
+            remote(far, far, 9, k, partner)
+
+    def spread(k):
+        arrived(block(k, SHARE[k], 4, 3, tile), 13, k)
+        mine = out.at[SHARE[k]:4, band, :, pl.ds(pl.multiple_of(k * width + zl * half, 128), half)]
         for n, r, t, device in xz_peers():
-            remote(mine, mine, 7, k, device)
-
-    def piece(k, yy, cc):
-        return out.at[:, pl.ds(pl.multiple_of(cc * 8, 8), 8), :, pl.ds(pl.multiple_of(k * width + yy * quarter, 128), quarter)]
-
-    def gather_y(k):
-        arrived(xin_like(k), 7, k)
-        mine = piece(k, y, c)
-        remote(mine, mine, 8, k, up)
-        remote(mine, mine, 11, k, down)
-        remote(mine, mine, 9, k, partner)
-
-    def forward(k):
-        whole = out.at[:, pl.ds(0, 8), :, pl.ds(0, quarter)]
-        arrived(whole, 8, k)
-        below = piece(k, lax.rem(y + 3, 4), c)
-        remote(below.at[pl.ds(0, 2)], below.at[pl.ds(0, 2)], 12, k, up)
-        remote(below, below, 9, k, partner)
-        arrived(whole, 11, k)
-        above = piece(k, lax.rem(y + 1, 4), c)
-        remote(above.at[pl.ds(2, 2)], above.at[pl.ds(2, 2)], 12, k, down)
-        remote(above, above, 9, k, partner)
-
-    def xin_like(k):
-        return out.at[:, pl.ds(0, 15), :, pl.ds(0, tile)]
-
-    def gather_core(k):
-        arrived(out.at[:, pl.ds(0, 8), :, pl.ds(0, quarter)], 12, k)
-        far = piece(k, lax.rem(y + 2, 4), c)
-        remote(far, far, 9, k, partner)
+            remote(mine, mine, 14, k, device)
+
+    def spread_core(k):
+        arrived(block(k, SHARE[k], 4, 15, half), 14, k)
+        mine = out.at[SHARE[k]:4, pl.ds(pl.multiple_of(c * 8, 8), 8), :, cols(k)]
+        remote(mine, mine, 15, k, partner)
 
     def finish():
-        whole = out.at[:, pl.ds(0, 8), :, pl.ds(0, quarter)]
         for k in range(CHUNKS):
             sent(ain[k].at[pl.ds(0, 15)], 0, k)
             sent(gb.at[k, pl.ds(0, 7)], 1, k)
@@ -258,12 +277,19 @@
             sent(ys.at[k], 5, k)
             sent(yin.at[k], 10, k)
             sent(xin.at[k], 6, k)
-            sent(xin_like(k), 7, k)
-            sent(whole, 8, k)
-            sent(whole, 11, k)
-            sent(whole, 12, k)
-            arrived(out.at[:, pl.ds(0, 8), :, pl.ds(0, width)], 9, k)
-            sent(out.at[:, pl.ds(0, 8), :, pl.ds(0, width)], 9, k)
+        for k in range(CHUNKS):
+            s = SHARE[k]
+            if s > 0:
+                sent(block(k, 0, s, 15, tile), 7, k)
+                for stage in (8, 11, 12):
+                    sent(block(k, 0, s, 8, 2 * tile), stage, k)
+                arrived(block(k, 0, s, 8, width), 9, k)
+                sent(block(k, 0, s, 8, width), 9, k)
+            if s < 4:
+                sent(block(k, s, 4, 3, tile), 13, k)
+                sent(block(k, s, 4, 15, half), 14, k)
+                arrived(block(k, s, 4, 8, width), 15, k)
+                sent(block(k, s, 4, 8, width), 15, k)
 
     def load():
         for k in range(CHUNKS):
@@ -272,7 +298,8 @@
 
     tab = []
     stages = dict(alpha=alpha, prefix=prefix, group=group, trans=trans, scale=scale, sum_core=sum_core, around=around, sum_y=sum_y,
-                  sum_xz=sum_xz, gather_y=gather_y, forward=forward, gather_core=gather_core)
+                  sum_xz=sum_xz, gather_y=gather_y, forward=forward, gather_core=gather_core, spread=spread,
+                  spread_core=spread_core)
     meet()
     for name in PLAN:
         with jax.named_scope(name):
@@ -291,7 +318,7 @@
 def local(images, depth, brick_map):
     channels, rows, columns = images.shape[1:]
     width = columns // CHUNKS
-    tile, quarter = width // 8, width // 4
+    tile, half = width // 8, width // 2
     f = jnp.float32
     n = CHUNKS
     vm = lambda *s: pltpu.VMEM(s, f)
@@ -304,9 +331,9 @@
             *[vm(16, ROW, width)] * n, *[vm(8, ROW, tile)] * n,
             vm(n, 16, ROW, width), vm(n, 8, ROW, tile), vm(n, 8, ROW, tile), vm(n, 8, ROW, tile), vm(n, 8, ROW, tile),
             vm(n, 16, ROW, width), vm(n, 16, ROW, width),
-            vm(n, 3, 16, ROW, width), vm(n, 3, 8, ROW, width), vm(n, 3, 8, ROW, width), vm(n, 3, 8, ROW, width),
-            vm(n, 2, 3, 4, ROW, quarter), vm(n, 2, 3, 4, ROW, quarter), vm(n, 2, 3, 8, ROW, quarter), vm(n, 3, 8, ROW, quarter), vm(n, 15, 3, ROW, tile),
-            pltpu.SemaphoreType.DMA((13, n)), pltpu.SemaphoreType.DMA((13, n)), pltpu.SemaphoreType.DMA((2, n)),
+            vm(n, 3, 16, ROW, width), vm(n, 3, 8, ROW, width), vm(n, 3, 8, ROW, width), vm(n, 3, 8, 2, ROW, half),
+            vm(n, 2, 3, 4, 2, ROW, tile), vm(n, 2, 3, 4, 2, ROW, tile), vm(n, 2, 3, 8, 2, ROW, tile), vm(n, 3, 8, 2, ROW, tile), vm(n, 15, 3, ROW, tile),
+            pltpu.SemaphoreType.DMA((16, n)), pltpu.SemaphoreType.DMA((16, n)), pltpu.SemaphoreType.DMA((2, n)),
         ],
         compiler_params=pltpu.CompilerParams(has_side_effects=True, collective_id=0, vmem_limit_bytes=48 * 2**20),
     )(depth, brick_map, images.reshape(channels, rows // ROW, ROW, columns))

time: 116 us -> 109 us (0.940)
  Pallas kernels: 112 us -> 106 us
    pallas_call x1, Pallas kernels: 112 us -> 106 us  [local(): pl.pallas_call(kernel, out_shape=pltpu.VMEM((channels, rows // ROW, ROW,...]
where the time goes in v4:
time: 109 us
  Pallas kernels  106 us (97%)
  local copies, waits for them, and re-layouts  3.4 us (3%)
    pallas_call x1, Pallas kernels, local(): pl.pallas_call(kernel, out_shape=pltpu.VMEM((channels, rows // ROW, ROW,...  106 us
    unnamed x1, local copies, waits for them, and re-layouts  3.4 us

profile of v4, /device:TPU:1, one launch (start us, length us, event | category | flops | bytes accessed | tf_op | source)
XLA Modules:
  0.0 109.2 jit_solution(5078990617234763435)
XLA Ops:
  0.0 105.8 %shard_map.37 = f32[4,16,8,4096]{3,2,1,0:T(8,128)S(1)} custom-call(s32[128]{0:T(128)} %depth.1, s32[128]{0:T(128)} %bricks.1, f32[4,16,8,4096]{3,2,1,0:T(8,128)} %bitcast.3), custom_call_target="tpu_custom_call" | custom-call | tf_op jit(solution)/shard_map/pallas_call | solution.py:325
  105.8 3.4 %copy.5 = f32[4,128,4096]{2,1,0:T(8,128)} copy(f32[4,128,4096]{2,1,0:T(8,128)S(1)} %bitcast.2) | data formatting | bytes 16777216

commit v5 on v4

--- a/solution.py
+++ b/solution.py
@@ -10,13 +10,12 @@
 
 AXES = ("zh", "x", "c", "zl", "y")
 CHUNKS = 4
-SHARE = (4, 3, 2, 2)
+SHARE = (4, 2, 2, 2)
 ROW = 8
 MESH = pl.DeviceIdType.MESH
 
-AA_ORDER = [(dx, dz, dc) for dc in (0, 1) for dx, dz in
-            ((1, 1), (3, 1), (0, 1), (2, 1), (1, 0), (3, 0), (2, 0), (0, 0))][:]
-AA_ORDER = [p for p in AA_ORDER if p != (0, 0, 0)]
+AA_ORDER = [(0, 0, 1), (0, 1, 0), (0, 1, 1), (1, 0, 0), (3, 1, 0), (2, 0, 0), (1, 1, 0), (3, 0, 0), (2, 1, 0),
+            (1, 0, 1), (3, 1, 1), (2, 0, 1), (1, 1, 1), (3, 0, 1), (2, 1, 1)]
 BA_ORDER = [(dy, dz) for dy in (2, 1, 3, 0) for dz in (1, 0) if (dy, dz) != (0, 0)]
 XZ_ORDER = [(dx, dz) for dx, dz in
             ((2, 2), (1, 2), (3, 2), (2, 1), (2, 3), (1, 1), (3, 3), (1, 3), (3, 1),
@@ -25,11 +24,11 @@
 PLAN = (
     "alpha0", "load", "alpha1", "prefix0", "alpha2", "group0", "prefix1", "alpha3", "group1", "prefix2",
     "trans0", "prefix3", "group2", "trans1", "scale0", "group3", "sum_core0", "trans2", "scale1", "around0",
-    "sum_core1", "trans3", "scale2", "around1", "sum_core2", "sum_y1", "sum_y0", "scale3", "around2",
-    "sum_core3", "sum_xz1", "sum_y2", "sum_xz0", "around3", "gather_y1", "sum_y3", "sum_xz2", "gather_y0",
-    "spread1", "sum_xz3", "gather_y2", "spread2", "forward1", "gather_y3", "forward2", "spread3",
-    "gather_core1", "spread_core1", "spread_core2", "forward0", "gather_core2", "forward3", "gather_core0",
-    "spread_core3", "gather_core3", "finish",
+    "sum_core1", "trans3", "scale2", "around1", "sum_y0", "sum_core2", "scale3", "around2", "sum_y1",
+    "sum_core3", "sum_xz0", "sum_xz1", "around3", "sum_y2", "gather_y0", "spread1", "sum_y3", "sum_xz2",
+    "gather_y1", "cross1", "sum_xz3", "forward0", "gather_y2", "spread2", "spread3", "spread_core1", "cross2",
+    "gather_y3", "gather_core0", "forward1", "cross3", "forward2", "spread_core2", "forward3", "gather_core1",
+    "spread_core3", "gather_core2", "gather_core3", "finish",
 )
 
 
@@ -102,14 +101,14 @@
         return pl.ds(k * width, width)
 
     def own_alpha(k):
-        return pltpu.make_async_copy(img.at[3, band, :, cols(k)], ain[k].at[band], own.at[0, k])
+        return pltpu.make_async_copy(img.at[3, c, zh, x, :, cols(k)], ain[k].at[band], own.at[0, k])
 
     def own_color(k):
-        return pltpu.make_async_copy(img.at[pl.ds(0, 3), :, :, cols(k)], col.at[k], own.at[1, k])
+        return pltpu.make_async_copy(img.at[0:3, :, :, :, :, cols(k)], col.at[k], own.at[1, k])
 
     def alpha(k, begin=0, end=15):
-        for r, device in list(aa_peers())[begin:end]:
-            remote(img.at[3, r, :, cols(k)], ain[k].at[band], 0, k, device)
+        for (zz, xx, cc, _, _), device in [(d, d) for _, d in aa_peers()][begin:end]:
+            remote(img.at[3, cc, zz, xx, :, cols(k)], ain[k].at[band], 0, k, device)
         if begin == 0:
             own_alpha(k).start()
 
@@ -132,7 +131,7 @@
         for m in range(8):
             qb[k, m] = run
             run = run * gin[k][tab[32 + m]]
-        out[3, band, :, pl.ds(pl.multiple_of(k * width + slot_b * tile, 128), tile)] = 1.0 - run
+        out[3, c, zh, x, :, strip(k)] = 1.0 - run
         for j in range(8):
             qout[k, j] = qb[k, tab[40 + j]]
         qin[k, slot_b] = qout[k, slot_b]
@@ -156,7 +155,7 @@
             r = (1 - c) * 8 + i
             t = tin[k, r]
             for ch in range(3):
-                cs[k, ch, i] = col[k, ch, r] * t
+                cs[k, ch, i] = col[k, ch, 1 - c, i // 4, i % 4] * t
             return carry
 
         lax.fori_loop(0, 8, body, 0)
@@ -169,7 +168,7 @@
             r = c * 8 + i
             t = tin[k, r]
             for ch in range(3):
-                v = col[k, ch, r] * t + cin[k, ch, i]
+                v = col[k, ch, c, i // 4, i % 4] * t + cin[k, ch, i]
                 a1[k, ch, i, 0] = v[:, :half]
                 a1[k, ch, i, 1] = v[:, half:]
             return carry
@@ -215,22 +214,22 @@
             v = a2[k, ch, zh * 4 + x, zl]
             for n in range(15):
                 v = v + xin[k, n, ch]
-            out[ch, band, :, strip(k)] = v
+            out[ch, c, zh, x, :, strip(k)] = v
         if SHARE[k] < 4:
-            mine = out.at[SHARE[k]:4, band, :, strip(k)]
+            mine = out.at[SHARE[k]:4, c, zh, x, :, strip(k)]
             for dy in (2, 1, 3):
                 remote(mine, mine, 13, k, (zh, x, c, zl, lax.rem(y + dy, 4)))
         if SHARE[k] > 0:
-            mine = out.at[0:SHARE[k], band, :, strip(k)]
+            mine = out.at[0:SHARE[k], c, zh, x, :, strip(k)]
             for n, r, t, device in xz_peers():
                 remote(mine, mine, 7, k, device)
 
     def block(k, first, last, count, columns):
-        return out.at[first:last, pl.ds(0, count), :, pl.ds(0, columns)]
+        return pre.at[0:last - first, 0:count, :, 0:columns]
 
     def piece(k, dy, h):
         at = pl.multiple_of(k * width + h * half + lax.rem(y + dy, 4) * tile, 128)
-        return out.at[0:SHARE[k], pl.ds(pl.multiple_of(c * 8, 8), 8), :, pl.ds(at, tile)]
+        return out.at[0:SHARE[k], c, :, :, :, pl.ds(at, tile)]
 
     def gather_y(k):
         arrived(block(k, 0, SHARE[k], 15, tile), 7, k)
@@ -258,13 +257,31 @@
 
     def spread(k):
         arrived(block(k, SHARE[k], 4, 3, tile), 13, k)
-        mine = out.at[SHARE[k]:4, band, :, pl.ds(pl.multiple_of(k * width + zl * half, 128), half)]
-        for n, r, t, device in xz_peers():
-            remote(mine, mine, 14, k, device)
+        for h in range(2):
+            mine = out.at[SHARE[k]:4, c, zh, x, :, columns(k, zl, h)]
+            for n in (2, 1, 3):
+                zz = lax.rem(z + n, 4)
+                device = (zz // 2, x, c, lax.rem(zz, 2), y) if h else (zh, lax.rem(x + n, 4), c, zl, y)
+                remote(mine, mine, 16 if h else 14, k, device)
+
+    def columns(k, zzl, h):
+        return pl.ds(pl.multiple_of(k * width + zzl * half + h * (half // 2), 128), half // 2)
+
+    def cross(k):
+        arrived(block(k, SHARE[k], 4, 3, half // 2), 14, k)
+        row = out.at[SHARE[k]:4, c, zh, :, :, columns(k, zl, 0)]
+        for n in (2, 1, 3):
+            zz = lax.rem(z + n, 4)
+            remote(row, row, 17, k, (zz // 2, x, c, lax.rem(zz, 2), y))
+        arrived(block(k, SHARE[k], 4, 3, half // 2), 16, k)
+        for n in (2, 1, 3):
+            for h in range(2):
+                line = out.at[SHARE[k]:4, c, :, x, :, columns(k, h, 1)]
+                remote(line, line, 17, k, (zh, lax.rem(x + n, 4), c, zl, y))
 
     def spread_core(k):
-        arrived(block(k, SHARE[k], 4, 15, half), 14, k)
-        mine = out.at[SHARE[k]:4, pl.ds(pl.multiple_of(c * 8, 8), 8), :, cols(k)]
+        arrived(block(k, SHARE[k], 4, 12, half), 17, k)
+        mine = out.at[SHARE[k]:4, c, :, :, :, cols(k)]
         remote(mine, mine, 15, k, partner)
 
     def finish():
@@ -287,7 +304,9 @@
                 sent(block(k, 0, s, 8, width), 9, k)
             if s < 4:
                 sent(block(k, s, 4, 3, tile), 13, k)
-                sent(block(k, s, 4, 15, half), 14, k)
+                sent(block(k, s, 4, 3, half // 2), 14, k)
+                sent(block(k, s, 4, 3, half // 2), 16, k)
+                sent(block(k, s, 4, 12, half), 17, k)
                 arrived(block(k, s, 4, 8, width), 15, k)
                 sent(block(k, s, 4, 8, width), 15, k)
 
@@ -298,7 +317,7 @@
 
     tab = []
     stages = dict(alpha=alpha, prefix=prefix, group=group, trans=trans, scale=scale, sum_core=sum_core, around=around, sum_y=sum_y,
-                  sum_xz=sum_xz, gather_y=gather_y, forward=forward, gather_core=gather_core, spread=spread,
+                  sum_xz=sum_xz, gather_y=gather_y, forward=forward, gather_core=gather_core, spread=spread, cross=cross,
                   spread_core=spread_core)
     meet()
     for name in PLAN:
@@ -324,19 +343,19 @@
     vm = lambda *s: pltpu.VMEM(s, f)
     out = pl.pallas_call(
         kernel,
-        out_shape=pltpu.VMEM((channels, rows // ROW, ROW, columns), f),
+        out_shape=pltpu.VMEM((channels, 2, 2, 4, ROW, columns), f),
         in_specs=[pl.BlockSpec(memory_space=pltpu.SMEM), pl.BlockSpec(memory_space=pltpu.SMEM), pl.BlockSpec(memory_space=pl.ANY)],
         out_specs=pl.BlockSpec(memory_space=pltpu.VMEM),
         scratch_shapes=[
             *[vm(16, ROW, width)] * n, *[vm(8, ROW, tile)] * n,
             vm(n, 16, ROW, width), vm(n, 8, ROW, tile), vm(n, 8, ROW, tile), vm(n, 8, ROW, tile), vm(n, 8, ROW, tile),
             vm(n, 16, ROW, width), vm(n, 16, ROW, width),
-            vm(n, 3, 16, ROW, width), vm(n, 3, 8, ROW, width), vm(n, 3, 8, ROW, width), vm(n, 3, 8, 2, ROW, half),
+            vm(n, 3, 2, 2, 4, ROW, width), vm(n, 3, 8, ROW, width), vm(n, 3, 8, ROW, width), vm(n, 3, 8, 2, ROW, half),
             vm(n, 2, 3, 4, 2, ROW, tile), vm(n, 2, 3, 4, 2, ROW, tile), vm(n, 2, 3, 8, 2, ROW, tile), vm(n, 3, 8, 2, ROW, tile), vm(n, 15, 3, ROW, tile),
-            pltpu.SemaphoreType.DMA((16, n)), pltpu.SemaphoreType.DMA((16, n)), pltpu.SemaphoreType.DMA((2, n)),
+            pltpu.SemaphoreType.DMA((18, n)), pltpu.SemaphoreType.DMA((18, n)), pltpu.SemaphoreType.DMA((2, n)),
         ],
         compiler_params=pltpu.CompilerParams(has_side_effects=True, collective_id=0, vmem_limit_bytes=48 * 2**20),
-    )(depth, brick_map, images.reshape(channels, rows // ROW, ROW, columns))
+    )(depth, brick_map, images.reshape(channels, 2, 2, 4, ROW, columns))
     return out.reshape(channels, rows, columns)
 
 

time: 109 us -> 104 us (0.954)
  Pallas kernels: 106 us -> 100 us
    pallas_call x1, Pallas kernels: 106 us -> 100 us  [local(): pl.pallas_call(kernel, out_shape=pltpu.VMEM((channels, 2, 2, 4, ROW, colu...]
where the time goes in v5:
time: 104 us
  Pallas kernels  100 us (96%)
  local copies, waits for them, and re-layouts  3.4 us (3%)
    pallas_call x1, Pallas kernels, local(): pl.pallas_call(kernel, out_shape=pltpu.VMEM((channels, 2, 2, 4, ROW, colu...  100 us
    unnamed x1, local copies, waits for them, and re-layouts  3.4 us

profile of v5, /device:TPU:1, one launch (start us, length us, event | category | flops | bytes accessed | tf_op | source)
XLA Modules:
  0.0 103.8 jit_solution(6210081039162650637)
XLA Ops:
  0.0 100.4 %shard_map.37 = f32[4,2,2,4,8,4096]{5,4,3,2,1,0:T(8,128)S(1)} custom-call(s32[128]{0:T(128)} %depth.1, s32[128]{0:T(128)} %bricks.1, f32[4,2,2,4,8,4096]{5,4,3,2,1,0:T(8,128)} %bitcast.3), custom_call_target="tpu_custom_call" | custom-call | tf_op jit(solution)/shard_map/pallas_call | solution.py:344
  100.4 3.4 %copy.5 = f32[4,128,4096]{2,1,0:T(8,128)} copy(f32[4,128,4096]{2,1,0:T(8,128)S(1)} %bitcast.2) | data formatting | bytes 16777216

commit v6 on v5

--- a/solution.py
+++ b/solution.py
@@ -1,4 +1,6 @@
 import functools
+import itertools
+import math
 
 import jax
 import jax.numpy as jnp
@@ -32,9 +34,9 @@
 )
 
 
-def kernel(depth, bricks, img, out, *scratch):
+def kernel(depth_in, bricks_in, img, out, *scratch):
     ain, gin = scratch[:CHUNKS], scratch[CHUNKS:2 * CHUNKS]
-    pre, gb, qb, qout, qin, tout, tin, col, cs, cin, a1, ys, b1, yin, a2, xin, send, recv, own = scratch[2 * CHUNKS:]
+    pre, gb, qb, qout, qin, tout, tin, col, cs, cin, a1, ys, b1, yin, a2, xin, send, recv, own, depth, bricks = scratch[2 * CHUNKS:]
     zh, x, c, zl, y = (lax.axis_index(a) for a in AXES)
     z = zh * 2 + zl
     width = tin.shape[-1]
@@ -45,15 +47,12 @@
 
     def remote(src, dst, stage, k, device):
         cp = pltpu.make_async_remote_copy(
-            src_ref=src, dst_ref=dst, send_sem=send.at[stage, k], recv_sem=recv.at[stage, k],
+            src_ref=src, dst_ref=dst, send_sem=send.at[stage], recv_sem=recv.at[stage, k],
             device_id=device, device_id_type=MESH)
         cp.start()
 
     def arrived(ref, stage, k):
         pltpu.make_async_copy(ref, ref, recv.at[stage, k]).wait()
-
-    def sent(ref, stage, k):
-        pltpu.make_async_copy(ref, ref, send.at[stage, k]).wait()
 
     def aa_peers():
         for dx, dz, dc in AA_ORDER:
@@ -284,41 +283,47 @@
         mine = out.at[SHARE[k]:4, c, :, :, :, cols(k)]
         remote(mine, mine, 15, k, partner)
 
+    def sent(count, stage):
+        for ref, most in ((pre, (CHUNKS, 16, 8)), (col, (CHUNKS, 3, 2, 2, 4, 8))):
+            for dims in itertools.product(*[range(1, m + 1) for m in most]):
+                if math.prod(dims) == count:
+                    ref = ref.at[tuple(slice(0, d) for d in dims[:-1]) + (slice(None), slice(0, dims[-1] * tile))]
+                    pltpu.make_async_copy(ref, ref, send.at[stage]).wait()
+                    return
+        assert count == 0
+
     def finish():
-        for k in range(CHUNKS):
-            sent(ain[k].at[pl.ds(0, 15)], 0, k)
-            sent(gb.at[k, pl.ds(0, 7)], 1, k)
-            sent(qout.at[k, pl.ds(0, 7)], 2, k)
-            sent(tout.at[k, pl.ds(0, 15)], 3, k)
-            sent(cs.at[k], 4, k)
-            sent(ys.at[k], 5, k)
-            sent(yin.at[k], 10, k)
-            sent(xin.at[k], 6, k)
         for k in range(CHUNKS):
             s = SHARE[k]
             if s > 0:
-                sent(block(k, 0, s, 15, tile), 7, k)
-                for stage in (8, 11, 12):
-                    sent(block(k, 0, s, 8, 2 * tile), stage, k)
                 arrived(block(k, 0, s, 8, width), 9, k)
-                sent(block(k, 0, s, 8, width), 9, k)
             if s < 4:
-                sent(block(k, s, 4, 3, tile), 13, k)
-                sent(block(k, s, 4, 3, half // 2), 14, k)
-                sent(block(k, s, 4, 3, half // 2), 16, k)
-                sent(block(k, s, 4, 12, half), 17, k)
                 arrived(block(k, s, 4, 8, width), 15, k)
-                sent(block(k, s, 4, 8, width), 15, k)
+        s = sum(SHARE)
+        rest = 4 * CHUNKS - s
+        once = {0: 15 * 8, 1: 7, 2: 7, 3: 15 * 8, 4: 3 * 8 * 8, 5: 2 * 3 * 4 * 2, 10: 2 * 3 * 8 * 2, 6: 15 * 3}
+        for stage, count in once.items():
+            sent(CHUNKS * count, stage)
+        for stage, count in {7: 15, 8: 16, 11: 16, 12: 16}.items():
+            sent(s * count, stage)
+        sent(s * 64, 9)
+        for stage, count in {13: 3, 14: 6, 16: 6, 17: 48, 15: 64}.items():
+            sent(rest * count, stage)
 
     def load():
         for k in range(CHUNKS):
             own_color(k).start()
+        for cp in ranks:
+            cp.wait()
         tab.extend(tables())
 
     tab = []
     stages = dict(alpha=alpha, prefix=prefix, group=group, trans=trans, scale=scale, sum_core=sum_core, around=around, sum_y=sum_y,
                   sum_xz=sum_xz, gather_y=gather_y, forward=forward, gather_core=gather_core, spread=spread, cross=cross,
                   spread_core=spread_core)
+    ranks = [pltpu.make_async_copy(depth_in, depth, own.at[2, 0]), pltpu.make_async_copy(bricks_in, bricks, own.at[2, 1])]
+    for cp in ranks:
+        cp.start()
     meet()
     for name in PLAN:
         with jax.named_scope(name):
@@ -344,7 +349,7 @@
     out = pl.pallas_call(
         kernel,
         out_shape=pltpu.VMEM((channels, 2, 2, 4, ROW, columns), f),
-        in_specs=[pl.BlockSpec(memory_space=pltpu.SMEM), pl.BlockSpec(memory_space=pltpu.SMEM), pl.BlockSpec(memory_space=pl.ANY)],
+        in_specs=[pl.BlockSpec(memory_space=pl.ANY)] * 3,
         out_specs=pl.BlockSpec(memory_space=pltpu.VMEM),
         scratch_shapes=[
             *[vm(16, ROW, width)] * n, *[vm(8, ROW, tile)] * n,
@@ -352,7 +357,8 @@
             vm(n, 16, ROW, width), vm(n, 16, ROW, width),
             vm(n, 3, 2, 2, 4, ROW, width), vm(n, 3, 8, ROW, width), vm(n, 3, 8, ROW, width), vm(n, 3, 8, 2, ROW, half),
             vm(n, 2, 3, 4, 2, ROW, tile), vm(n, 2, 3, 4, 2, ROW, tile), vm(n, 2, 3, 8, 2, ROW, tile), vm(n, 3, 8, 2, ROW, tile), vm(n, 15, 3, ROW, tile),
-            pltpu.SemaphoreType.DMA((18, n)), pltpu.SemaphoreType.DMA((18, n)), pltpu.SemaphoreType.DMA((2, n)),
+            pltpu.SemaphoreType.DMA((18,)), pltpu.SemaphoreType.DMA((18, n)), pltpu.SemaphoreType.DMA((3, n)),
+            pltpu.SMEM(depth.shape, jnp.int32), pltpu.SMEM(brick_map.shape, jnp.int32),
         ],
         compiler_params=pltpu.CompilerParams(has_side_effects=True, collective_id=0, vmem_limit_bytes=48 * 2**20),
     )(depth, brick_map, images.reshape(channels, 2, 2, 4, ROW, columns))

time: 104 us -> 103 us (level)
  no operation moved by 1% of the time
where the time goes in v6:
time: 103 us
  Pallas kernels  99.5 us (97%)
  local copies, waits for them, and re-layouts  3.4 us (3%)
    pallas_call x1, Pallas kernels, local(): pl.pallas_call(kernel, out_shape=pltpu.VMEM((channels, 2, 2, 4, ROW, colu...  99.5 us
    unnamed x1, local copies, waits for them, and re-layouts  3.4 us

profile of v6, /device:TPU:1, one launch (start us, length us, event | category | flops | bytes accessed | tf_op | source)
XLA Modules:
  0.0 102.9 jit_solution(670874820780377248)
XLA Ops:
  0.0 99.5 %shard_map.37 = f32[4,2,2,4,8,4096]{5,4,3,2,1,0:T(8,128)S(1)} custom-call(s32[128]{0:T(128)} %depth_in.1, s32[128]{0:T(128)} %bricks_in.1, f32[4,2,2,4,8,4096]{5,4,3,2,1,0:T(8,128)} %bitcast.3), custom_call_target="tpu_custom_call" | custom-call | tf_op jit(solution)/shard_map/pallas_call | solution.py:349
  99.5 3.4 %copy.5 = f32[4,128,4096]{2,1,0:T(8,128)} copy(f32[4,128,4096]{2,1,0:T(8,128)S(1)} %bitcast.2) | data formatting | bytes 16777216

commit v7 on v6

--- a/solution.py
+++ b/solution.py
@@ -26,9 +26,9 @@
 PLAN = (
     "alpha0", "load", "alpha1", "prefix0", "alpha2", "group0", "prefix1", "alpha3", "group1", "prefix2",
     "trans0", "prefix3", "group2", "trans1", "scale0", "group3", "sum_core0", "trans2", "scale1", "around0",
-    "sum_core1", "trans3", "scale2", "around1", "sum_y0", "sum_core2", "scale3", "around2", "sum_y1",
-    "sum_core3", "sum_xz0", "sum_xz1", "around3", "sum_y2", "gather_y0", "spread1", "sum_y3", "sum_xz2",
-    "gather_y1", "cross1", "sum_xz3", "forward0", "gather_y2", "spread2", "spread3", "spread_core1", "cross2",
+    "sum_core1", "trans3", "scale2", "around1", "sum_core2", "sum_y0", "scale3", "sum_y1", "around2",
+    "sum_xz0", "sum_core3", "sum_xz1", "around3", "sum_y2", "gather_y0", "spread1", "sum_y3", "sum_xz2",
+    "gather_y1", "cross1", "spread2", "sum_xz3", "forward0", "gather_y2", "spread3", "spread_core1", "cross2",
     "gather_y3", "gather_core0", "forward1", "cross3", "forward2", "spread_core2", "forward3", "gather_core1",
     "spread_core3", "gather_core2", "gather_core3", "finish",
 )

time: 103 us -> 102 us (level)
  no operation moved by 1% of the time
where the time goes in v7:
time: 102 us
  Pallas kernels  98.8 us (97%)
  local copies, waits for them, and re-layouts  3.4 us (3%)
    pallas_call x1, Pallas kernels, local(): pl.pallas_call(kernel, out_shape=pltpu.VMEM((channels, 2, 2, 4, ROW, colu...  98.8 us
    unnamed x1, local copies, waits for them, and re-layouts  3.4 us

profile of v7, /device:TPU:1, one launch (start us, length us, event | category | flops | bytes accessed | tf_op | source)
XLA Modules:
  0.0 102.2 jit_solution(12087931398755519332)
XLA Ops:
  0.0 98.8 %shard_map.37 = f32[4,2,2,4,8,4096]{5,4,3,2,1,0:T(8,128)S(1)} custom-call(s32[128]{0:T(128)} %depth_in.1, s32[128]{0:T(128)} %bricks_in.1, f32[4,2,2,4,8,4096]{5,4,3,2,1,0:T(8,128)} %bitcast.3), custom_call_target="tpu_custom_call" | custom-call | tf_op jit(solution)/shard_map/pallas_call | solution.py:349
  98.8 3.4 %copy.5 = f32[4,128,4096]{2,1,0:T(8,128)} copy(f32[4,128,4096]{2,1,0:T(8,128)S(1)} %bitcast.2) | data formatting | bytes 16777216

commit v8 on v7

--- a/solution.py
+++ b/solution.py
@@ -47,7 +47,7 @@
 
     def remote(src, dst, stage, k, device):
         cp = pltpu.make_async_remote_copy(
-            src_ref=src, dst_ref=dst, send_sem=send.at[stage], recv_sem=recv.at[stage, k],
+            src_ref=src, dst_ref=dst, send_sem=send.at[stage], recv_sem=recv.at[stage, 0 if stage in (9, 15) else k],
             device_id=device, device_id_type=MESH)
         cp.start()
 
@@ -76,9 +76,9 @@
 
     def meet():
         barrier = pltpu.get_barrier_semaphore()
-        devices = [d for _, d in aa_peers()] + [d for _, d in ba_peers()]
-        devices += [(zz // 2, xx, c, lax.rem(zz, 2), y) for xx, zz in
-                    ((lax.rem(x + dx, 4), lax.rem(z + dz, 4)) for dx in range(4) for dz in (1, 3))]
+        devices = [(zz // 2, xx, c, lax.rem(zz, 2), y) for xx, zz in
+                    ((lax.rem(x + dx, 4), lax.rem(z + dz, 4)) for dx in (2, 1, 3, 0) for dz in (3, 1))]
+        devices = [d for _, d in aa_peers()][::-1] + devices + [d for _, d in ba_peers()]
         for device in devices:
             pl.semaphore_signal(barrier, inc=1, device_id=device, device_id_type=MESH)
         pl.semaphore_wait(barrier, len(devices))
@@ -283,24 +283,20 @@
         mine = out.at[SHARE[k]:4, c, :, :, :, cols(k)]
         remote(mine, mine, 15, k, partner)
 
-    def sent(count, stage):
+    def sent(count, stage, sem=None):
         for ref, most in ((pre, (CHUNKS, 16, 8)), (col, (CHUNKS, 3, 2, 2, 4, 8))):
             for dims in itertools.product(*[range(1, m + 1) for m in most]):
                 if math.prod(dims) == count:
                     ref = ref.at[tuple(slice(0, d) for d in dims[:-1]) + (slice(None), slice(0, dims[-1] * tile))]
-                    pltpu.make_async_copy(ref, ref, send.at[stage]).wait()
+                    pltpu.make_async_copy(ref, ref, send.at[stage] if sem is None else sem).wait()
                     return
         assert count == 0
 
     def finish():
-        for k in range(CHUNKS):
-            s = SHARE[k]
-            if s > 0:
-                arrived(block(k, 0, s, 8, width), 9, k)
-            if s < 4:
-                arrived(block(k, s, 4, 8, width), 15, k)
         s = sum(SHARE)
         rest = 4 * CHUNKS - s
+        sent(s * 64, 9, recv.at[9, 0])
+        sent(rest * 64, 15, recv.at[15, 0])
         once = {0: 15 * 8, 1: 7, 2: 7, 3: 15 * 8, 4: 3 * 8 * 8, 5: 2 * 3 * 4 * 2, 10: 2 * 3 * 8 * 2, 6: 15 * 3}
         for stage, count in once.items():
             sent(CHUNKS * count, stage)

time: 102 us -> 103 us (level)
  no operation moved by 1% of the time
where the time goes in v8:
time: 103 us
  Pallas kernels  99.2 us (96%)
  local copies, waits for them, and re-layouts  3.4 us (3%)
    pallas_call x1, Pallas kernels, local(): pl.pallas_call(kernel, out_shape=pltpu.VMEM((channels, 2, 2, 4, ROW, colu...  99.2 us
    unnamed x1, local copies, waits for them, and re-layouts  3.4 us

profile of v8, /device:TPU:1, one launch (start us, length us, event | category | flops | bytes accessed | tf_op | source)
XLA Modules:
  0.0 102.6 jit_solution(7539692888625410622)
XLA Ops:
  0.0 99.2 %shard_map.37 = f32[4,2,2,4,8,4096]{5,4,3,2,1,0:T(8,128)S(1)} custom-call(s32[128]{0:T(128)} %depth_in.1, s32[128]{0:T(128)} %bricks_in.1, f32[4,2,2,4,8,4096]{5,4,3,2,1,0:T(8,128)} %bitcast.3), custom_call_target="tpu_custom_call" | custom-call | tf_op jit(solution)/shard_map/pallas_call | solution.py:345
  99.2 3.4 %copy.5 = f32[4,128,4096]{2,1,0:T(8,128)} copy(f32[4,128,4096]{2,1,0:T(8,128)S(1)} %bitcast.2) | data formatting | bytes 16777216
